TPU v7x, 32 devices: a whole 2x2x4 slice. The times are simulated.
32 devices in a mesh: gx: 4 (over x, core), gy: 4 (over z), gz: 2 (over y).
Axes of the slice: x: 2, y: 2, z: 4, core: 2. Of those that a mesh axis runs over, the one named last changes fastest.
Arguments:
- fields: float32 [11, 500, 32, 256], P(None, 'gx', 'gy', 'gz'), may hold values from -6 to 6
- var_scale: float32 [11], replicated, may hold values from 0.3 to 3
- start_basis: float32 [500, 64], replicated, may hold values from -6 to 6
Outputs:
- factor: float32 [500, 64], replicated
- core: float32 [64, 11, 32, 256], P('gx', None, 'gy', 'gz')
All inputs are finite; a program needn't handle non-finite values.
Results may differ from a plain program's by a relative error of at most 0.0002.
Values sent between devices are 32-bit elements; how exact they have to be, the bound alone decides.
No kernel may reach another device: no remote copies, remote signals or barrier semaphores. Data moves between devices by JAX's collectives and lax.ppermute only.
A program may use at most 128 MiB of HBM per device.

v0:
```python
import jax
import jax.numpy as jnp
from jax import lax
from jax.sharding import PartitionSpec as P

ITERS = 3


def orthonormal(block):
    small = jnp.dot(block.T, block, precision=lax.Precision.HIGHEST)
    lower = jnp.linalg.cholesky(small)
    return jax.scipy.linalg.solve_triangular(lower, block.T, lower=True).T


def per_device(fields, var_scale, start_basis):
    scaled = fields * var_scale[:, None, None, None]
    rows_dev = scaled.shape[1]
    contract = (((0, 2, 3), (0, 2, 3)), ((), ()))
    swapped = lax.all_to_all(scaled, "gx", split_axis=2, concat_axis=1, tiled=True)
    partial_gram = lax.dot_general(swapped, swapped, contract, precision=lax.Precision.HIGHEST)
    gram = lax.psum(partial_gram, ("gx", "gy", "gz"))
    basis = start_basis
    for step in range(ITERS):
        basis = orthonormal(jnp.dot(gram, basis, precision=lax.Precision.HIGHEST))
    along_rows = (((0,), (1,)), ((), ()))
    own_basis = lax.dynamic_slice_in_dim(basis, lax.axis_index("gx") * rows_dev, rows_dev, 0)
    core = lax.psum_scatter(
        lax.dot_general(own_basis, scaled, along_rows, precision=lax.Precision.HIGHEST),
        "gx",
        scatter_dimension=0,
        tiled=True,
    )
    return (basis, core)


def solution(mesh):
    in_specs = (P(None, "gx", "gy", "gz"), P(), P())
    out_specs = (P(), P("gx", None, "gy", "gz"))
    return jax.shard_map(
        per_device, mesh=mesh, in_specs=in_specs, out_specs=out_specs, check_vma=False
    )
```

profile of v0, /device:TPU:0, one launch (start us, length us, event | category | flops | bytes accessed | tf_op | source)
XLA Modules:
  0.0 333.2 jit_solution(15597270235788873526)
XLA Ops:
  7.2 3.1 broadcast_multiply_fusion
  10.3 1.1 copy.24
  11.4 1.3 copy-done.1
  12.7 69.0 %all_to_all.18 = f32[11,125,8,128]{3,1,0,2:T(8,128)S(1)} all-to-all(f32[11,125,8,128]{3,1,0,2:T(8,128)S(1)} %copy.24), channel_id=1, replica_groups=mesh['gx'=4,'gy'=4,'gz'=2] {'gx'}, dimensions={2} | all-to-all | bytes 11264000 | tf_op jit(solution)/shard_map/all_to_all | solution.py:19
  81.7 2.9 copy.36
  84.6 6.2 %all_to_all.16 = f32[11,500,2,128]{3,1,2,0:T(8,128)} reshape(f32[11,4,125,2,128]{4,2,1,3,0:T(8,128)} %bitcast.67) | data formatting | bytes 11264000 | tf_op jit(solution)/shard_map/all_to_all | solution.py:19
  90.8 13.6 %convolution_bitcast_fusion = f32[500,500]{1,0:T(8,128)} fusion(f32[11,500,2,128]{3,1,2,0:T(8,128)} %all_to_all.16), kind=kOutput, calls=%fused_computation.4 | convolution fusion | flops 8448000000 | bytes 6632000 | tf_op jit(solution)/shard_map/dot_general | solution.py:20
  104.7 130.7 %all-reduce.2.cloned.1.call-done = f32[500,500]{1,0:T(8,128)} async-done(((f32[500,500]{1,0:T(8,128)}), f32[500,500]{1,0:T(8,128)}) %all-reduce.2.cloned.1.call-update) | async-done | bytes 1000016 | tf_op jit(solution)/shard_map/psum | solution.py:21
  235.4 2.3 fusion.24
  237.7 0.3 fusion.25
  238.0 5.8 %cholesky.59 = f32[64,64]{1,0:T(8,128)S(1)} custom-call(f32[64,64]{1,0:T(8,128)S(1)} %fusion.17), custom_call_target="Cholesky" | custom-call | tf_op jit(solution)/shard_map/jit(cholesky)/cholesky | solution.py:11
  243.9 0.6 compare_reduce_fusion.2
  244.6 0.7 fusion.8
  245.2 4.9 %custom-call.7 = f32[1,64,64]{1,2,0:T(8,128)S(1)} custom-call(f32[1,64,64]{2,1,0:T(8,128)S(1)} %fusion.8), custom_call_target="InvertDiagBlocksLowerTriangular" | custom-call | tf_op jit(solution)/shard_map/jit(_solve_triangular)/triangular_solve | solution.py:12
  250.1 0.3 fusion.6
  250.5 2.3 fusion.26
  252.8 0.3 fusion.27
  253.1 5.8 %cholesky.70 = f32[64,64]{1,0:T(8,128)S(1)} custom-call(f32[64,64]{1,0:T(8,128)S(1)} %fusion.15), custom_call_target="Cholesky" | custom-call | tf_op jit(solution)/shard_map/jit(cholesky)/cholesky | solution.py:11
  259.0 0.6 compare_reduce_fusion.1
  259.6 0.7 fusion.9
  260.3 4.9 %custom-call.8 = f32[1,64,64]{1,2,0:T(8,128)S(1)} custom-call(f32[1,64,64]{2,1,0:T(8,128)S(1)} %fusion.9), custom_call_target="InvertDiagBlocksLowerTriangular" | custom-call | tf_op jit(solution)/shard_map/jit(_solve_triangular)/triangular_solve | solution.py:12
  265.2 0.3 fusion.4
  265.5 2.3 fusion.28
  267.8 0.3 fusion.29
  268.2 5.8 %cholesky.81 = f32[64,64]{1,0:T(8,128)S(1)} custom-call(f32[64,64]{1,0:T(8,128)S(1)} %fusion.13), custom_call_target="Cholesky" | custom-call | tf_op jit(solution)/shard_map/jit(cholesky)/cholesky | solution.py:11
  274.1 0.6 compare_reduce_fusion
  274.7 0.7 fusion.10
  275.4 4.9 %custom-call.9 = f32[1,64,64]{1,2,0:T(8,128)S(1)} custom-call(f32[1,64,64]{2,1,0:T(8,128)S(1)} %fusion.10), custom_call_target="InvertDiagBlocksLowerTriangular" | custom-call | tf_op jit(solution)/shard_map/jit(_solve_triangular)/triangular_solve | solution.py:12
  280.3 0.3 fusion.2
  280.6 8.3 %fusion = f32[64,11,8,128]{3,0,2,1:T(8,128)} fusion(f32[11,125,8,128]{3,2,1,0:T(8,128)} %copy-done.1, f32[64,500]{1,0:T(8,128)S(1)} %fusion.2, s32[]{:T(128)S(6)} %select_n.6), kind=kOutput, calls=%fused_computation | convolution fusion | flops 1081344000 | bytes 8548356 | tf_op jit(solution)/shard_map/dot_general | solution.py:28
  288.9 35.2 %reduce-scatter.2.cloned.1.call-done = f32[16,11,8,128]{3,0,2,1:T(8,128)} async-done(((f32[64,11,8,128]{3,0,2,1:T(8,128)}), f32[16,11,8,128]{3,0,2,1:T(8,128)}) %reduce-scatter.2.cloned.1.call-update) | async-done | bytes 720912 | tf_op jit(solution)/shard_map/reduce_scatter | solution.py:27
  324.2 2.2 copy.30
  (18 shorter events, 0.7 us)
Async XLA Ops:
  7.2 228.2 %copy-start = (f32[500,64]{0,1:T(8,128)S(1)}, f32[500,64]{0,1:T(8,128)}, u32[]{:S(2)}) copy-start(f32[500,64]{0,1:T(8,128)} %param.8) | copy-start | bytes 384004
  7.2 228.2 %all-reduce.2.cloned.1.call-start = ((), (), s32[]{:S(2)}) async-start(), calls=%async_computation.2 | async-start | bytes 2064384 | tf_op jit(solution)/shard_map/psum | solution.py:21
  10.3 2.4 copy-start.1
  104.4 219.7 %reduce-scatter.2.cloned.1.call-start = ((), (), s32[]{:S(2)}) async-start(), calls=%async_computation.3 | async-start | bytes 3604480 | tf_op jit(solution)/shard_map/reduce_scatter | solution.py:27
  280.6 8.3 %copy-start.2 = (f32[64,500]{1,0:T(8,128)}, f32[64,500]{1,0:T(8,128)S(1)}, u32[]{:S(2)}) copy-start(f32[64,500]{1,0:T(8,128)S(1)} %fusion.2) | copy-start | bytes 384004
Sparse Core Ops, SparseCore 0:
  104.6 130.7 all-reduce.1
  289.0 35.0 reduce-scatter.1
where the time goes:
time: 334 us; the launch traced here: 333 us
  waiting for transfers between devices  166 us (50%)
  blocking collectives  69 us (21%)
  other arithmetic  39.3 us (12%)
  matrix products  30.5 us (9%)
  between operations  14.2 us (4%)
  local copies, waits for them, and re-layouts  13.9 us (4%)
    psum x1, waiting for transfers between devices, per_device(): gram = lax.psum(partial_gram, ('gx', 'gy', 'gz'))  131 us
    all_to_all x1, blocking collectives, per_device(): lax.all_to_all(scaled, 'gx', split_axis=2, concat_axis=1, tiled=True)  69 us
    reduce_scatter x1, waiting for transfers between devices, per_device(): lax.psum_scatter(lax.dot_general(own_basis, scaled, along_rows, precision...  35.2 us
    another operation x9, other arithmetic, orthonormal(): lower = jnp.linalg.cholesky(small)  19.6 us
    another operation x6, other arithmetic, orthonormal(): return jax.scipy.linalg.solve_triangular(lower, block.T, lower=True).T  16.6 us
    dot_general x1, matrix products, per_device(): lax.dot_general(swapped, swapped, contract, precision=lax.Precision.HIGHEST)  13.6 us
    all_to_all x2, local copies, waits for them, and re-layouts, per_device(): lax.all_to_all(scaled, 'gx', split_axis=2, concat_axis=1, tiled=True)  9.05 us
    dot_general x1, matrix products, per_device(): lax.dot_general(own_basis, scaled, along_rows, precision=lax.Precision.HI...  8.26 us
  transfers between devices with their start and end apart: 2, of which 2 were waited for; matrix products, arithmetic and copies ran while one was open for 0% of the time, Pallas kernels for 0%

commit v1 on v0

v1 whole, which is shorter than its diff:
```python
import jax
import jax.numpy as jnp
from jax import lax
from jax.sharding import PartitionSpec as P

ITERS = 3
LANE = 128
CHUNKS = 2
HIGH = lax.Precision.HIGH
HIGHEST = lax.Precision.HIGHEST


def swap(array, axis, size, step):
    return lax.ppermute(array, axis, [(i, i ^ step) for i in range(size)])


def orthonormal(block):
    small = jnp.dot(block.T, block, precision=HIGHEST)
    lower = jnp.linalg.cholesky(small)
    return jax.scipy.linalg.solve_triangular(lower, block.T, lower=True).T


def outer(left, right):
    return lax.dot_general(left, right, (((0, 2), (0, 2)), ((), ())), precision=HIGH)


def solution(mesh):
    sizes = dict(mesh.shape)
    nx = sizes["gx"]
    chip = nx // 2

    def sum_columns(part):
        for axis in ("gz", "gy"):
            step = 1
            while step < sizes[axis]:
                part = part + swap(part, axis, sizes[axis], step)
                step *= 2
        return part

    def in_order(mine, me):
        near = swap(mine, "gx", nx, 1)
        far = swap(mine, "gx", nx, chip)
        both = swap(far, "gx", nx, 1)
        stack = jnp.stack([mine, near, far, both])
        return jnp.stack([lax.dynamic_index_in_dim(stack, me ^ g, 0, keepdims=False) for g in range(nx)])

    def per_device(fields, var_scale, start_basis):
        v, rows, j, k = fields.shape
        rank = start_basis.shape[1]
        keep = rank // nx
        pad = -(-rows // LANE) * LANE
        me = lax.axis_index("gx")
        x = me // chip
        scaled = fields * var_scale[:, None, None, None]
        tall = jnp.pad(scaled.transpose(2, 0, 1, 3), ((0, 0), (0, 0), (0, pad - rows), (0, 0)))
        half = j // 2

        def half_of(array, which):
            return lax.dynamic_slice_in_dim(array, which * half, half, 0).reshape(half * v, -1, k)

        ours = half_of(tall, x)
        theirs = half_of(tall, 1 - x)
        cut = pad // CHUNKS
        far = [swap(theirs[:, q * cut:(q + 1) * cut], "gx", nx, chip) for q in range(CHUNKS)]
        near = swap(tall, "gx", nx, 1)
        whole = tall.reshape(j * v, pad, k)
        diag = sum_columns(jnp.stack([outer(whole, whole), outer(near.reshape(j * v, pad, k), whole)]))
        near_half = half_of(near, x)
        cross = [sum_columns(jnp.stack([outer(ours, f), outer(near_half, f)])) for f in far]
        cross = jnp.concatenate(cross, axis=2)
        diag, cross = in_order(diag, me), in_order(cross, me)
        rows_of = []
        for b in range(nx):
            blocks = [None] * nx
            blocks[b] = diag[b, 0]
            blocks[b ^ 1] = diag[b ^ 1, 1]
            blocks[b ^ chip] = cross[b, 0] + cross[b ^ chip, 0].T
            blocks[b ^ chip ^ 1] = cross[b ^ 1, 1] + cross[b ^ chip, 1].T
            rows_of.append(jnp.concatenate(blocks, axis=1))
        gram = jnp.concatenate(rows_of, axis=0)
        basis = jnp.pad(start_basis.reshape(nx, rows, rank), ((0, 0), (0, pad - rows), (0, 0))).reshape(nx * pad, rank)
        for step in range(ITERS):
            basis = orthonormal(jnp.dot(gram, basis, precision=HIGHEST))
        basis = basis.reshape(nx, pad, rank)
        far = jnp.concatenate(far, axis=1)
        both = swap(far, "gx", nx, 1)
        held = [ours, near_half, far, both]

        def ranks(which):
            out = 0.0
            for s, data in enumerate((0, 1, chip, chip ^ 1)):
                own = lax.dynamic_index_in_dim(basis, me ^ data, 0, keepdims=False)
                own = lax.dynamic_slice_in_dim(own, which * keep, keep, 1)
                out = out + lax.dot_general(own, held[s], (((0,), (1,)), ((), ())), precision=HIGH)
            return out

        got = swap(ranks(me ^ chip), "gx", nx, chip)
        kept = ranks(me)
        low = jnp.where(x == 0, kept, got)
        high = jnp.where(x == 0, got, kept)
        core = jnp.concatenate([low, high], axis=1).reshape(keep, j, v, k).transpose(0, 2, 1, 3)
        return basis[:, :rows].reshape(nx * rows, rank), core

    in_specs = (P(None, "gx", "gy", "gz"), P(), P())
    out_specs = (P(), P("gx", None, "gy", "gz"))
    return jax.shard_map(per_device, mesh=mesh, in_specs=in_specs, out_specs=out_specs, check_vma=False)
```

time: 334 us -> 228 us (0.68)
  waiting for transfers between devices: 166 us -> 69 us
  blocking collectives: 69 us -> 0 us
  local copies, waits for them, and re-layouts: 13.9 us -> 40.4 us
  matrix products: 30.5 us -> 50.5 us
  starting transfers between devices: 0.26 us -> 18.9 us
  between operations: 14.2 us -> 1.08 us
  other arithmetic: 39.3 us -> 47.1 us
    psum x1 -> x0, waiting for transfers between devices: 131 us -> none  [per_device(): gram = lax.psum(partial_gram, ('gx', 'gy', 'gz'))]
    ppermute x0 -> x20, waiting for transfers between devices: none -> 69 us  [swap(): return lax.ppermute(array, axis, [(i, i ^ step) for i in range(size)])]
    all_to_all x1 -> x0, blocking collectives: 69 us -> none  [per_device(): lax.all_to_all(scaled, 'gx', split_axis=2, concat_axis=1, tiled=True)]
    reduce_scatter x1 -> x0, waiting for transfers between devices: 35.2 us -> none  [per_device(): lax.psum_scatter(lax.dot_general(own_basis, scaled, along_rows, precision...]
    dot_general x8 -> x20, matrix products: 29.5 us -> 49.5 us  [the longest x6 28.3 us: outer(): lax.dot_general(left, right, (((0, 2), (0, 2)), ((), ())), precision=HIGH)]
    ppermute x0 -> x20, starting transfers between devices: none -> 18.9 us  [swap(): return lax.ppermute(array, axis, [(i, i ^ step) for i in range(size)])]
    dynamic_slice x0 -> x6, local copies, waits for them, and re-layouts: none -> 13.1 us  [the longest x5 13.1 us: half_of(): lax.dynamic_slice_in_dim(array, which * half, half, 0)]
    all_to_all x2 -> x0, local copies, waits for them, and re-layouts: 9.05 us -> none  [per_device(): lax.all_to_all(scaled, 'gx', split_axis=2, concat_axis=1, tiled=True)]
  transfers between devices with their start and end apart: 2 -> 20, of which waited for: 2 -> 11; matrix products, arithmetic and copies ran while one was open for 0% -> 49% of each run, Pallas kernels for 0% -> 0%
where the time goes in v1:
time: 228 us; the launch traced here: 227 us
  waiting for transfers between devices  69 us (30%)
  matrix products  50.5 us (22%)
  other arithmetic  47.1 us (21%)
  local copies, waits for them, and re-layouts  40.4 us (18%)
  starting transfers between devices  18.9 us (8%)
    ppermute x20, waiting for transfers between devices, swap(): return lax.ppermute(array, axis, [(i, i ^ step) for i in range(size)])  69 us
    dot_general x6, matrix products, outer(): lax.dot_general(left, right, (((0, 2), (0, 2)), ((), ())), precision=HIGH)  28.3 us
    another operation x9, other arithmetic, orthonormal(): lower = jnp.linalg.cholesky(small)  19.7 us
    ppermute x20, starting transfers between devices, swap(): return lax.ppermute(array, axis, [(i, i ^ step) for i in range(size)])  18.9 us
    another operation x6, other arithmetic, orthonormal(): return jax.scipy.linalg.solve_triangular(lower, block.T, lower=True).T  16.6 us
    dot_general x8, matrix products, ranks(): lax.dot_general(own, held[s], (((0,), (1,)), ((), ())), precision=HIGH)  15.6 us
    dynamic_slice x5, local copies, waits for them, and re-layouts, half_of(): lax.dynamic_slice_in_dim(array, which * half, half, 0)  13.1 us
    unnamed x21, local copies, waits for them, and re-layouts  8.35 us
  transfers between devices with their start and end apart: 20, of which 11 were waited for; matrix products, arithmetic and copies ran while one was open for 49% of the time, Pallas kernels for 0%

profile of v1, /device:TPU:0, one launch (start us, length us, event | category | flops | bytes accessed | tf_op | source)
XLA Modules:
  0.0 227.1 jit_solution(6296307992806039737)
XLA Ops:
  0.6 3.0 %multiply_bitcast_fusion = f32[8,11,125,128]{3,0,2,1:T(8,128)S(1)} fusion(f32[11,125,8,128]{3,2,1,0:T(8,128)} %param.6, f32[11]{0:T(128)} %param.7), kind=kLoop, calls=%fused_computation.2 | loop fusion | flops 1408000 | bytes 11264044 | tf_op jit(solution)/shard_map/transpose | solution.py:55
  3.7 3.3 %pad.8 = f32[8,11,128,128]{3,0,2,1:T(8,128)} pad(f32[8,11,125,128]{3,0,2,1:T(8,128)S(1)} %multiply_bitcast_fusion, f32[]{:T(128)} %constant.218.clone.1), padding=0_0x0_0x0_3x0_0 | pad | bytes 11399172 | tf_op jit(solution)/shard_map/jit(_pad)/pad | solution.py:55
  8.3 6.9 %constant_dynamic-slice_fusion.15 = (f32[4,11,128,128]{3,0,2,1:T(4,128)}, f32[4,11,128,128]{3,0,2,1:T(4,128)S(1)}) fusion(s32[]{:T(128)S(6)} %select_n.80, f32[8,11,125,128]{3,0,2,1:T(8,128)} %copy-done.3, s32[]{:T(128)S(6)} %select_n.81), kind=kLoop, calls=%fused_computation.91 | loop fusion | bytes 11399176 | tf_op jit(solution)/shard_map/dynamic_slice | solution.py:59
  17.5 2.5 %collective-permute-start.11 = (f32[44,64,128]{2,1,0:T(8,128)}, f32[44,64,128]{2,1,0:T(8,128)}, u32[]{:S(2)}, u32[]{:S(2)}) collective-permute-start(f32[44,64,128]{2,1,0:T(8,128)} %get-tuple-element.7), channel_id=1, source_target_pairs={{0,16},{8,24},{16,0},{24,8},{1,17},{9,25},{17,1},{25,9},{2,18},{10... | collective-permute-start | bytes 4325384 | tf_op jit(solution)/shard_map/ppermute | solution.py:14
  20.0 2.2 copy.50
  23.1 8.3 %fusion.7 = f32[1,128,128]{1,2,0:T(8,128)S(1)} fusion(f32[8,11,128,128]{3,0,2,1:T(8,128)} %pad.8), kind=kOutput, calls=%fused_computation.13 | convolution fusion | flops 1107296256 | bytes 5832704 | tf_op jit(solution)/shard_map/dot_general | solution.py:24
  31.4 21.4 %collective-permute-done.11 = f32[44,64,128]{2,1,0:T(8,128)} collective-permute-done((f32[44,64,128]{2,1,0:T(8,128)}, f32[44,64,128]{2,1,0:T(8,128)}, u32[]{:S(2)}, u32[]{:S(2)}) %collective-permute-start.11) | collective-permute-done | bytes 1441824 | tf_op jit(solution)/shard_map/ppermute | solution.py:14
  52.8 2.6 %convolution_bitcast_fusion.2 = f32[1,128,64]{2,1,0:T(8,128)S(1)} fusion(f32[44,128,128]{2,1,0:T(8,128)S(1)} %bitcast.195, f32[44,64,128]{2,1,0:T(8,128)} %collective-permute-done.11), kind=kOutput, calls=%fused_computation.16 | convolution fusion | flops 276824064 | bytes 4358144 | tf_op jit(solution)/shard_map/dot_general | solution.py:24
  55.4 28.1 %collective-permute-done.7 = f32[44,64,128]{2,1,0:T(8,128)} collective-permute-done((f32[44,64,128]{2,1,0:T(8,128)}, f32[44,64,128]{2,1,0:T(8,128)}, u32[]{:S(2)}, u32[]{:S(2)}) %collective-permute-start.7) | collective-permute-done | bytes 1441824 | tf_op jit(solution)/shard_map/ppermute | solution.py:14
  83.5 2.6 %convolution_bitcast_fusion.4 = f32[1,128,64]{2,1,0:T(8,128)S(1)} fusion(f32[44,128,128]{2,1,0:T(8,128)S(1)} %bitcast.196, f32[44,64,128]{2,1,0:T(8,128)} %collective-permute-done.7), kind=kOutput, calls=%fused_computation.18 | convolution fusion | flops 276824064 | bytes 4358144 | tf_op jit(solution)/shard_map/dot_general | solution.py:24
  86.1 8.5 %fusion.10 = f32[1,128,128]{1,2,0:T(8,128)S(1)} fusion(f32[8,11,128,128]{3,0,2,1:T(8,128)} %pad.8, f32[8,11,128,128]{3,0,2,1:T(8,128)} %collective-permute-done), kind=kOutput, calls=%fused_computation.14 | convolution fusion | flops 1107296256 | bytes 11599872 | tf_op jit(solution)/shard_map/dot_general | solution.py:24
  96.5 3.3 %constant_dynamic-slice_fusion.13 = f32[4,11,128,128]{3,0,2,1:T(4,128)S(1)} fusion(f32[8,11,128,128]{3,0,2,1:T(8,128)} %collective-permute-done, s32[]{:T(128)S(6)} %select_n.80), kind=kLoop, calls=%fused_computation.89 | loop fusion | bytes 5767172 | tf_op jit(solution)/shard_map/dynamic_slice | solution.py:59
  100.1 3.7 %convolution_bitcast_fusion.1 = f32[1,128,64]{2,1,0:T(8,128)S(1)} fusion(f32[44,128,128]{2,1,0:T(8,128)S(1)} %bitcast.199, f32[44,64,128]{2,1,0:T(8,128)} %collective-permute-done.11), kind=kOutput, calls=%fused_computation.15 | convolution fusion | flops 276824064 | bytes 4358144 | tf_op jit(solution)/shard_map/dot_general | solution.py:24
  104.1 2.6 %convolution_bitcast_fusion.3 = f32[1,128,64]{2,1,0:T(8,128)S(1)} fusion(f32[44,128,128]{2,1,0:T(8,128)S(1)} %bitcast.200, f32[44,64,128]{2,1,0:T(8,128)} %collective-permute-done.7), kind=kOutput, calls=%fused_computation.17 | convolution fusion | flops 276824064 | bytes 4358144 | tf_op jit(solution)/shard_map/dot_general | solution.py:24
  115.1 2.7 %collective-permute-start.14 = (f32[2,128,64]{2,1,0:T(8,128)S(1)}, f32[2,128,64]{2,1,0:T(8,128)S(1)}, u32[]{:S(2)}, u32[]{:S(2)}) collective-permute-start(f32[2,128,64]{2,1,0:T(8,128)S(1)} %fusion.85), channel_id=1, source_target_pairs={{0,4},{2,6},{4,0},{6,2},{1,5},{3,7},{5,1},{7,3},{8,12},{10,14},{12... | collective-permute-start | bytes 196616 | tf_op jit(solution)/shard_map/ppermute | solution.py:14
  117.8 3.4 %collective-permute-done.9 = f32[2,128,64]{2,1,0:T(8,128)S(1)} collective-permute-done((f32[2,128,64]{2,1,0:T(8,128)S(1)}, f32[2,128,64]{2,1,0:T(8,128)S(1)}, u32[]{:S(2)}, u32[]{:S(2)}) %collective-permute-start.9) | collective-permute-done | bytes 65568 | tf_op jit(solution)/shard_map/ppermute | solution.py:14
  121.9 2.7 %constant_dynamic-update-slice_fusion.1 = f32[44,128,128]{2,1,0:T(8,128)} fusion(f32[44,64,128]{2,1,0:T(8,128)} %collective-permute-done.7), kind=kLoop, calls=%fused_computation.95 | loop fusion | bytes 2883584
  124.6 2.6 %collective-permute-done.14 = f32[2,128,64]{2,1,0:T(8,128)S(1)} collective-permute-done((f32[2,128,64]{2,1,0:T(8,128)S(1)}, f32[2,128,64]{2,1,0:T(8,128)S(1)}, u32[]{:S(2)}, u32[]{:S(2)}) %collective-permute-start.14) | collective-permute-done | bytes 65568 | tf_op jit(solution)/shard_map/ppermute | solution.py:14
  130.5 3.3 %collective-permute-done.16 = f32[2,128,128]{2,1,0:T(8,128)S(1)} collective-permute-done((f32[2,128,128]{2,1,0:T(8,128)S(1)}, f32[2,128,128]{2,1,0:T(8,128)S(1)}, u32[]{:S(2)}, u32[]{:S(2)}) %collective-permute-start.16) | collective-permute-done | bytes 131104 | tf_op jit(solution)/shard_map/ppermute | solution.py:14
  133.8 2.7 %constant_dynamic-update-slice_fusion = f32[44,128,128]{2,1,0:T(8,128)} fusion(f32[44,128,128]{2,1,0:T(8,128)} %constant_dynamic-update-slice_fusion.1, f32[44,64,128]{2,1,0:T(8,128)} %collective-permute-done.11), kind=kLoop, calls=%fused_computation.94 | loop fusion | bytes 2883584 | tf_op jit(solution)/shard_map/concatenate | solution.py:85
  137.0 3.1 %collective-permute-done.3 = f32[2,128,128]{1,2,0:T(8,128)S(1)} collective-permute-done((f32[2,128,128]{1,2,0:T(8,128)S(1)}, f32[2,128,128]{1,2,0:T(8,128)S(1)}, u32[]{:S(2)}, u32[]{:S(2)}) %collective-permute-start.3) | collective-permute-done | bytes 131104 | tf_op jit(solution)/shard_map/ppermute | solution.py:14
  161.6 5.8 %cholesky.59 = f32[64,64]{1,0:T(8,128)S(1)} custom-call(f32[64,64]{1,0:T(8,128)S(1)} %fusion.31), custom_call_target="Cholesky" | custom-call | tf_op jit(solution)/shard_map/jit(cholesky)/cholesky | solution.py:19
  168.8 4.9 %custom-call.7 = f32[1,64,64]{1,2,0:T(8,128)S(1)} custom-call(f32[1,64,64]{2,1,0:T(8,128)S(1)} %fusion.23), custom_call_target="InvertDiagBlocksLowerTriangular" | custom-call | tf_op jit(solution)/shard_map/jit(_solve_triangular)/triangular_solve | solution.py:20
  176.4 6.0 %cholesky.70 = f32[64,64]{1,0:T(8,128)S(1)} custom-call(f32[64,64]{1,0:T(8,128)S(1)} %fusion.29), custom_call_target="Cholesky" | custom-call | tf_op jit(solution)/shard_map/jit(cholesky)/cholesky | solution.py:19
  183.8 4.9 %custom-call.8 = f32[1,64,64]{1,2,0:T(8,128)S(1)} custom-call(f32[1,64,64]{2,1,0:T(8,128)S(1)} %fusion.24), custom_call_target="InvertDiagBlocksLowerTriangular" | custom-call | tf_op jit(solution)/shard_map/jit(_solve_triangular)/triangular_solve | solution.py:20
  191.4 5.8 %cholesky.81 = f32[64,64]{1,0:T(8,128)S(1)} custom-call(f32[64,64]{1,0:T(8,128)S(1)} %fusion.27), custom_call_target="Cholesky" | custom-call | tf_op jit(solution)/shard_map/jit(cholesky)/cholesky | solution.py:19
  198.6 4.9 %custom-call.9 = f32[1,64,64]{1,2,0:T(8,128)S(1)} custom-call(f32[1,64,64]{2,1,0:T(8,128)S(1)} %fusion.25), custom_call_target="InvertDiagBlocksLowerTriangular" | custom-call | tf_op jit(solution)/shard_map/jit(_solve_triangular)/triangular_solve | solution.py:20
  206.6 2.6 %fusion.48 = f32[16,44,128]{2,0,1:T(8,128)S(1)} fusion(f32[128,16,1]{0,1,2:T(8,128)S(1)} %bitcast.222, f32[44,128,128]{2,1,0:T(8,128)} %collective-permute-done.18), kind=kOutput, calls=%fused_computation.111 | convolution fusion | flops 69206016 | bytes 3252224 | tf_op jit(solution)/shard_map/dot_general | solution.py:94
  209.3 3.4 %fusion.6 = f32[16,44,128]{2,0,1:T(8,128)} fusion(f32[16,44,128]{2,0,1:T(8,128)S(1)} %fusion.48, f32[16,44,128]{2,0,1:T(8,128)S(1)} %convolution_add_fusion.1, f32[128,16,1]{0,1,2:T(8,128)S(1)} %bitcast.221, f32[44,128,128]{2,1,0:T(8,128)} %constant_dynamic-update-slice_fusion), kind=kOutput, calls=%fused_computation.11 | convolution fusion | flops 69386240 | bytes 3973120 | tf_op jit(solution)/shard_map/dot_general | solution.py:94
  215.0 3.5 %fusion.46 = f32[16,44,128]{2,0,1:T(8,128)} fusion(f32[128,16,1]{0,1,2:T(8,128)S(1)} %bitcast.219, f32[44,128,128]{2,1,0:T(8,128)} %collective-permute-done.18), kind=kOutput, calls=%fused_computation.109 | convolution fusion | flops 69206016 | bytes 3252224 | tf_op jit(solution)/shard_map/dot_general | solution.py:94
  220.1 3.2 %collective-permute-done.19 = f32[16,44,128]{2,0,1:T(8,128)} collective-permute-done((f32[16,44,128]{2,0,1:T(8,128)}, f32[16,44,128]{2,0,1:T(8,128)}, u32[]{:S(2)}, u32[]{:S(2)}) %collective-permute-start.19) | collective-permute-done | bytes 360480 | tf_op jit(solution)/shard_map/ppermute | solution.py:14
  223.3 2.7 %broadcast_select_fusion.1 = (f32[16,44,128]{2,0,1:T(8,128)S(1)}, f32[16,44,128]{2,0,1:T(8,128)S(1)}) fusion(f32[16,44,128]{2,0,1:T(8,128)} %collective-permute-done.19, pred[]{:T(512)S(6)} %eq.4, f32[16,44,128]{2,0,1:T(8,128)S(1)} %copy-done.5, f32[16,44,128]{2,0,1:T(8,128)S(1)} %convolution_add_fusion.3, f32[128,16,1]{0,1,2:T(8,128)S(1)} %bitcast.217, ...), kind=kOutput, calls=%fused_computation.27 | convolution fusion | flops 69566464 | bytes 4694017 | tf_op jit(solution)/shard_map/dot_general | solution.py:94
  (117 shorter events, 58.8 us)
Async XLA Ops:
  3.7 4.2 %copy-start.3 = (f32[8,11,125,128]{3,0,2,1:T(8,128)}, f32[8,11,125,128]{3,0,2,1:T(8,128)S(1)}, u32[]{:S(2)}) copy-start(f32[8,11,125,128]{3,0,2,1:T(8,128)S(1)} %multiply_bitcast_fusion) | copy-start | bytes 16896004
  7.8 78.3 %collective-permute-start = (f32[8,11,128,128]{3,0,2,1:T(8,128)}, f32[8,11,128,128]{3,0,2,1:T(8,128)}, u32[]{:S(2)}, u32[]{:S(2)}) collective-permute-start(f32[8,11,128,128]{3,0,2,1:T(8,128)} %pad.8), channel_id=1, source_target_pairs={{0,8},{8,0},{16,24},{24,16},{1,9},{9,1},{17,25},{25,17},{2,10},{10... | collective-permute-start | bytes 17301512 | tf_op jit(solution)/shard_map/ppermute | solution.py:14
  17.5 35.2 %collective-permute-start.11 = (f32[44,64,128]{2,1,0:T(8,128)}, f32[44,64,128]{2,1,0:T(8,128)}, u32[]{:S(2)}, u32[]{:S(2)}) collective-permute-start(f32[44,64,128]{2,1,0:T(8,128)} %get-tuple-element.7), channel_id=1, source_target_pairs={{0,16},{8,24},{16,0},{24,8},{1,17},{9,25},{17,1},{25,9},{2,18},{10... | collective-permute-start | bytes 4325384 | tf_op jit(solution)/shard_map/ppermute | solution.py:14
  20.0 63.5 %collective-permute-start.7 = (f32[44,64,128]{2,1,0:T(8,128)}, f32[44,64,128]{2,1,0:T(8,128)}, u32[]{:S(2)}, u32[]{:S(2)}) collective-permute-start(f32[44,64,128]{2,1,0:T(8,128)} %get-tuple-element.6), channel_id=1, source_target_pairs={{0,16},{8,24},{16,0},{24,8},{1,17},{9,25},{17,1},{25,9},{2,18},{10... | collective-permute-start | bytes 4325384 | tf_op jit(solution)/shard_map/ppermute | solution.py:14
  20.0 2.2 copy-start.7
  94.6 19.2 %collective-permute-start.1 = (f32[2,128,128]{1,2,0:T(8,128)S(1)}, f32[2,128,128]{1,2,0:T(8,128)S(1)}, u32[]{:S(2)}, u32[]{:S(2)}) collective-permute-start(f32[2,128,128]{1,2,0:T(8,128)S(1)} %pad_maximum_fusion.5), channel_id=1, source_target_pairs={{0,1},{1,0},{2,3},{3,2},{4,5},{5,4},{6,7},{7,6},{8,9},{9,8},{10,11... | collective-permute-start | bytes 393224 | tf_op jit(solution)/shard_map/ppermute | solution.py:14
  100.1 6.7 %copy-start = (f32[4,11,128,128]{3,2,1,0:T(8,128)}, f32[4,11,128,128]{3,2,1,0:T(8,128)S(1)}, u32[]{:S(2)}) copy-start(f32[4,11,128,128]{3,2,1,0:T(8,128)S(1)} %copy.53) | copy-start | bytes 8650756
  103.8 5.0 %collective-permute-start.12 = (f32[2,128,64]{2,1,0:T(8,128)S(1)}, f32[2,128,64]{2,1,0:T(8,128)S(1)}, u32[]{:S(2)}, u32[]{:S(2)}) collective-permute-start(f32[2,128,64]{2,1,0:T(8,128)S(1)} %pad_maximum_fusion.7), channel_id=1, source_target_pairs={{0,1},{1,0},{2,3},{3,2},{4,5},{5,4},{6,7},{7,6},{8,9},{9,8},{10,11... | collective-permute-start | bytes 196616 | tf_op jit(solution)/shard_map/ppermute | solution.py:14
  106.8 5.0 %collective-permute-start.8 = (f32[2,128,64]{2,1,0:T(8,128)S(1)}, f32[2,128,64]{2,1,0:T(8,128)S(1)}, u32[]{:S(2)}, u32[]{:S(2)}) collective-permute-start(f32[2,128,64]{2,1,0:T(8,128)S(1)} %pad_maximum_fusion.6), channel_id=1, source_target_pairs={{0,1},{1,0},{2,3},{3,2},{4,5},{5,4},{6,7},{7,6},{8,9},{9,8},{10,11... | collective-permute-start | bytes 196616 | tf_op jit(solution)/shard_map/ppermute | solution.py:14
  108.9 6.2 %collective-permute-start.13 = (f32[2,128,64]{2,1,0:T(8,128)S(1)}, f32[2,128,64]{2,1,0:T(8,128)S(1)}, u32[]{:S(2)}, u32[]{:S(2)}) collective-permute-start(f32[2,128,64]{2,1,0:T(8,128)S(1)} %fusion.36), channel_id=1, source_target_pairs={{0,2},{2,0},{4,6},{6,4},{1,3},{3,1},{5,7},{7,5},{8,10},{10,8},{12,... | collective-permute-start | bytes 196616 | tf_op jit(solution)/shard_map/ppermute | solution.py:14
  111.9 9.3 %collective-permute-start.9 = (f32[2,128,64]{2,1,0:T(8,128)S(1)}, f32[2,128,64]{2,1,0:T(8,128)S(1)}, u32[]{:S(2)}, u32[]{:S(2)}) collective-permute-start(f32[2,128,64]{2,1,0:T(8,128)S(1)} %fusion.37), channel_id=1, source_target_pairs={{0,2},{2,0},{4,6},{6,4},{1,3},{3,1},{5,7},{7,5},{8,10},{10,8},{12,... | collective-permute-start | bytes 196616 | tf_op jit(solution)/shard_map/ppermute | solution.py:14
  113.8 16.6 %collective-permute-start.2 = (f32[2,128,128]{1,2,0:T(8,128)S(1)}, f32[2,128,128]{1,2,0:T(8,128)S(1)}, u32[]{:S(2)}, u32[]{:S(2)}) collective-permute-start(f32[2,128,128]{1,2,0:T(8,128)S(1)} %fusion.38), channel_id=1, source_target_pairs={{0,2},{2,0},{4,6},{6,4},{1,3},{3,1},{5,7},{7,5},{8,10},{10,8},{12,... | collective-permute-start | bytes 393224 | tf_op jit(solution)/shard_map/ppermute | solution.py:14
  115.1 12.1 %collective-permute-start.14 = (f32[2,128,64]{2,1,0:T(8,128)S(1)}, f32[2,128,64]{2,1,0:T(8,128)S(1)}, u32[]{:S(2)}, u32[]{:S(2)}) collective-permute-start(f32[2,128,64]{2,1,0:T(8,128)S(1)} %fusion.85), channel_id=1, source_target_pairs={{0,4},{2,6},{4,0},{6,2},{1,5},{3,7},{5,1},{7,3},{8,12},{10,14},{12... | collective-permute-start | bytes 196616 | tf_op jit(solution)/shard_map/ppermute | solution.py:14
  121.3 7.4 %collective-permute-start.10 = (f32[2,128,64]{2,1,0:T(8,128)S(1)}, f32[2,128,64]{2,1,0:T(8,128)S(1)}, u32[]{:S(2)}, u32[]{:S(2)}) collective-permute-start(f32[2,128,64]{2,1,0:T(8,128)S(1)} %fusion.84), channel_id=1, source_target_pairs={{0,4},{2,6},{4,0},{6,2},{1,5},{3,7},{5,1},{7,3},{8,12},{10,14},{12... | collective-permute-start | bytes 196616 | tf_op jit(solution)/shard_map/ppermute | solution.py:14
  128.8 5.0 %collective-permute-start.16 = (f32[2,128,128]{2,1,0:T(8,128)S(1)}, f32[2,128,128]{2,1,0:T(8,128)S(1)}, u32[]{:S(2)}, u32[]{:S(2)}) collective-permute-start(f32[2,128,128]{2,1,0:T(8,128)S(1)} %pad_maximum_fusion.8), channel_id=1, source_target_pairs={{0,16},{8,24},{16,0},{24,8},{1,17},{9,25},{17,1},{25,9},{2,18},{10... | collective-permute-start | bytes 393224 | tf_op jit(solution)/shard_map/ppermute | solution.py:14
  130.4 10.9 %collective-permute-start.15 = (f32[2,128,128]{2,1,0:T(8,128)S(1)}, f32[2,128,128]{2,1,0:T(8,128)S(1)}, u32[]{:S(2)}, u32[]{:S(2)}) collective-permute-start(f32[2,128,128]{2,1,0:T(8,128)S(1)} %pad_maximum_fusion.8), channel_id=1, source_target_pairs={{0,8},{8,0},{16,24},{24,16},{1,9},{9,1},{17,25},{25,17},{2,10},{10... | collective-permute-start | bytes 393224 | tf_op jit(solution)/shard_map/ppermute | solution.py:14
  130.4 9.7 %collective-permute-start.3 = (f32[2,128,128]{1,2,0:T(8,128)S(1)}, f32[2,128,128]{1,2,0:T(8,128)S(1)}, u32[]{:S(2)}, u32[]{:S(2)}) collective-permute-start(f32[2,128,128]{1,2,0:T(8,128)S(1)} %fusion.86), channel_id=1, source_target_pairs={{0,4},{2,6},{4,0},{6,2},{1,5},{3,7},{5,1},{7,3},{8,12},{10,14},{12... | collective-permute-start | bytes 393224 | tf_op jit(solution)/shard_map/ppermute | solution.py:14
  133.8 7.5 %collective-permute-start.17 = (f32[2,128,128]{2,1,0:T(8,128)S(1)}, f32[2,128,128]{2,1,0:T(8,128)S(1)}, u32[]{:S(2)}, u32[]{:S(2)}) collective-permute-start(f32[2,128,128]{2,1,0:T(8,128)S(1)} %collective-permute-done.16), channel_id=1, source_target_pairs={{0,8},{8,0},{16,24},{24,16},{1,9},{9,1},{17,25},{25,17},{2,10},{10... | collective-permute-start | bytes 393224 | tf_op jit(solution)/shard_map/ppermute | solution.py:14
  136.5 70.2 %collective-permute-start.18 = (f32[44,128,128]{2,1,0:T(8,128)}, f32[44,128,128]{2,1,0:T(8,128)}, u32[]{:S(2)}, u32[]{:S(2)}) collective-permute-start(f32[44,128,128]{2,1,0:T(8,128)} %constant_dynamic-update-slice_fusion), channel_id=1, source_target_pairs={{0,8},{8,0},{16,24},{24,16},{1,9},{9,1},{17,25},{25,17},{2,10},{10... | collective-permute-start | bytes 8650760 | tf_op jit(solution)/shard_map/ppermute | solution.py:14
  140.7 8.6 %collective-permute-start.5 = (f32[2,128,128]{1,2,0:T(8,128)}, f32[2,128,128]{1,2,0:T(8,128)}, u32[]{:S(2)}, u32[]{:S(2)}) collective-permute-start(f32[2,128,128]{1,2,0:T(8,128)} %add.154), channel_id=1, source_target_pairs={{0,16},{8,24},{16,0},{24,8},{1,17},{9,25},{17,1},{25,9},{2,18},{10... | collective-permute-start | bytes 393224 | tf_op jit(solution)/shard_map/ppermute | solution.py:14
  141.2 10.1 %collective-permute-start.4 = (f32[2,128,128]{1,2,0:T(8,128)}, f32[2,128,128]{1,2,0:T(8,128)}, u32[]{:S(2)}, u32[]{:S(2)}) collective-permute-start(f32[2,128,128]{1,2,0:T(8,128)} %add.154), channel_id=1, source_target_pairs={{0,8},{8,0},{16,24},{24,16},{1,9},{9,1},{17,25},{25,17},{2,10},{10... | collective-permute-start | bytes 393224 | tf_op jit(solution)/shard_map/ppermute | solution.py:14
  149.3 2.1 collective-permute-start.6
  152.4 8.0 %copy-start.6 = (f32[4,128,64]{1,0,2:T(4,128)S(1)}, f32[4,128,64]{1,0,2:T(4,128)}, u32[]{:S(2)}) copy-start(f32[4,128,64]{1,0,2:T(4,128)} %pad.9) | copy-start | bytes 393220
  159.4 1.0 copy-start.4
  203.8 1.8 copy-start.1
  212.6 10.6 %collective-permute-start.19 = (f32[16,44,128]{2,0,1:T(8,128)}, f32[16,44,128]{2,0,1:T(8,128)}, u32[]{:S(2)}, u32[]{:S(2)}) collective-permute-start(f32[16,44,128]{2,0,1:T(8,128)} %fusion.6), channel_id=1, source_target_pairs={{0,16},{8,24},{16,0},{24,8},{1,17},{9,25},{17,1},{25,9},{2,18},{10... | collective-permute-start | bytes 1081352 | tf_op jit(solution)/shard_map/ppermute | solution.py:14
  215.0 4.3 %copy-start.2 = (f32[4,11,128,128]{3,2,1,0:T(8,128)S(1)}, f32[4,11,128,128]{3,2,1,0:T(8,128)}, u32[]{:S(2)}) copy-start(f32[4,11,128,128]{3,2,1,0:T(8,128)} %copy-done) | copy-start | bytes 8650756
  219.3 4.0 %copy-start.5 = (f32[16,44,128]{2,0,1:T(8,128)S(1)}, f32[16,44,128]{2,0,1:T(8,128)}, u32[]{:S(2)}) copy-start(f32[16,44,128]{2,0,1:T(8,128)} %fusion.46) | copy-start | bytes 1081348

commit v2 on v0

v2 whole, which is shorter than its diff:
```python
import jax
import jax.numpy as jnp
from jax import lax
from jax.experimental import pallas as pl
from jax.experimental.pallas import tpu as pltpu
from jax.sharding import PartitionSpec as P


ITERS = 3
LANE = 128
SUB = 8
V_EARLY = 4
V_LATE = 8
TAIL = 4
RATE = 1e9
PACK_MIB = (59, 50)
DIAG_MIB = 8
CROSS_MIB = 8
SOLVE_MIB = 16
HIGHEST = lax.Precision.HIGHEST
F32 = jnp.float32
BF16 = jnp.bfloat16
NT = (((1,), (1,)), ((), ()))
NN = (((1,), (0,)), ((), ()))


def split(x):
    high = x.astype(BF16)
    return high, (x - high.astype(F32)).astype(BF16)


def mm(a, b, dims):
    return lax.dot_general(a, b, dims, preferred_element_type=F32)


def vmem():
    return pl.BlockSpec(memory_space=pltpu.VMEM)


def smem():
    return pl.BlockSpec(memory_space=pltpu.SMEM)


def fill(out, spot, buf, a, scale, first, step, count, half, width):
    tail = count // SUB * SUB
    for j in range(half):
        lanes = slice((spot * half + j) * width, (spot * half + j + 1) * width)
        if tail < out.shape[0]:
            out[tail:, lanes] = jnp.zeros((out.shape[0] - tail, width), F32)
        out[:count, lanes] = buf[a, pl.ds(first + j, count, stride=step), :] * scale


def limit(mib):
    return pltpu.CompilerParams(vmem_limit_bytes=mib * 1024 * 1024)


def cost(micros):
    return pl.CostEstimate(flops=int(micros * RATE), bytes_accessed=0, transcendentals=0)


def pack(fields, scale, x, rows, pad, j, whole):
    v, _, width = fields.shape
    half, cut = j // 2, pad - pad // TAIL
    early = V_EARLY
    count = v if whole else early

    def body(x_ref, s_ref, f_ref, *refs):
        *outs, buf, sems = refs
        span = rows if whole else cut
        copies = [
            pltpu.make_async_copy(f_ref.at[a, pl.ds(0, span * j)], buf.at[a], sems.at[a]) for a in range(count)
        ]
        for copy in copies:
            copy.start()
        other = (1 - x_ref[0]) * half
        for a in range(count):
            copies[a].wait()
            if not whole:
                fill(outs[0], a, buf, a, s_ref[a], other, j, cut, half, width)
                continue
            late, low, high, ours = outs
            if a >= early:
                fill(late, a - early, buf, a, s_ref[a], other, j, cut, half, width)
            piece, b = (low, a) if a < V_LATE else (high, a - V_LATE)
            fill(piece, b, buf, a, s_ref[a], cut * j + other, j, rows - cut, half, width)
            fill(ours, a, buf, a, s_ref[a], x_ref[0] * half, j, rows, half, width)

    def shape(n, height):
        return jax.ShapeDtypeStruct((height, n * half * width), F32)

    shapes = [shape(early, cut)]
    if whole:
        shapes = [shape(v - early, cut), shape(V_LATE, pad - cut), shape(v - V_LATE, pad - cut), shape(v, pad)]
    return pl.pallas_call(
        body,
        out_shape=shapes,
        in_specs=[smem(), smem(), pl.BlockSpec(memory_space=pltpu.HBM)],
        out_specs=[vmem()] * len(shapes),
        scratch_shapes=[
            pltpu.VMEM((count, (rows if whole else cut) * j, width), F32),
            pltpu.SemaphoreType.DMA((count,)),
        ],
        cost_estimate=cost(5 if whole else 2),
        compiler_params=limit(PACK_MIB[whole]),
        name="pack_rest" if whole else "pack_first",
    )(x, scale, fields)


def diagonal(ours, theirs, near_ours, near_theirs, v):
    pad, total = ours.shape
    width = total // v

    def body(o_ref, a1, a2, b1, b2, n_ref, c1, c2, d1, d2, high, low, diag):
        diag[...] = jnp.zeros_like(diag)

        def at(a):
            return pl.ds(pl.multiple_of(a * width, width), width)

        def add(own, near):
            own, near = split(own), split(near)
            chip_high = jnp.concatenate([own[0], near[0]], 0)
            chip_low = jnp.concatenate([own[1], near[1]], 0)
            high_t, low_t = chip_high.T, chip_low.T
            both = mm(jnp.concatenate(own, 0), high_t, NN)
            diag[...] += both[:pad] + both[pad:] + mm(own[0], low_t, NN)
            return chip_high, chip_low

        def mine(a, carry):
            lanes = at(a)
            high[:, lanes], low[:, lanes] = add(o_ref[:, lanes], n_ref[:, lanes])
            return carry

        lax.fori_loop(0, v, mine, 0)
        for first, last in segments(v):
            p = (a1, c1, 0) if first < V_EARLY else (a2, c2, V_EARLY)
            q = (b1, d1, 0) if first < V_LATE else (b2, d2, V_LATE)

            def other(a, carry, p=p, q=q):
                top, bottom = at(a - p[2]), at(a - q[2])
                own = jnp.concatenate([p[0][:, top], q[0][:, bottom]], 0)
                add(own, jnp.concatenate([p[1][:, top], q[1][:, bottom]], 0))
                return carry

            lax.fori_loop(first, last, other, 0)

    half = jax.ShapeDtypeStruct((2 * pad, total), BF16)
    return pl.pallas_call(
        body,
        out_shape=(half, half, jax.ShapeDtypeStruct((pad, 2 * pad), F32)),
        in_specs=[vmem()] * 10,
        out_specs=(vmem(),) * 3,
        cost_estimate=cost(12),
        compiler_params=limit(DIAG_MIB),
        name="diagonal",
    )(ours, *theirs, near_ours, *near_theirs)


def segments(v):
    edges = sorted({0, V_EARLY, V_LATE, v})
    return list(zip(edges[:-1], edges[1:]))


def crossing(high, low, pieces, base, first):
    cut = pieces[0].shape[0]
    pad = high.shape[0] // 2

    def body(h_ref, l_ref, *refs):
        out = refs[-1]
        spot = first
        total = 0.0
        for ref in refs[:len(pieces)]:
            lanes = slice(spot, spot + ref.shape[1])
            top, bottom = split(ref[...].T)
            both = mm(h_ref[:, lanes], jnp.concatenate([top, bottom], 1), NN)
            total = total + both[:, :cut] + both[:, cut:] + mm(l_ref[:, lanes], top, NN)
            spot += ref.shape[1]
        total = total.T
        out[...] = total if base is None else refs[-2][...] + total

    extra = [] if base is None else [base]
    return pl.pallas_call(
        body,
        out_shape=jax.ShapeDtypeStruct((cut, 2 * pad), F32),
        in_specs=[vmem()] * (2 + len(pieces) + len(extra)),
        out_specs=vmem(),
        cost_estimate=cost(3),
        compiler_params=limit(CROSS_MIB),
        name="crossing",
    )(high, low, *pieces, *extra)


def inverse_factor(work, out, rank):
    for p in range(rank // SUB):
        top = p * SUB
        lane = rank + top
        groups = range(p + 1, rank // SUB)
        cols = {}
        for g in groups:
            tile = work[g * SUB:(g + 1) * SUB, :]
            for k in range(SUB):
                cols[g, k] = jnp.broadcast_to(tile[:, lane + k:lane + k + 1], (SUB, 2 * rank))
        rows = [work[pl.ds(top + k, SUB, stride=0), :] for k in range(SUB)]
        small = {}
        for a in range(SUB):
            for b in range(a + 1):
                small[a, b] = jnp.broadcast_to(rows[a][:, lane + b:lane + b + 1], (SUB, 2 * rank))
        for k in range(SUB):
            pivot = small[k, k]
            inv = 1.0 / pivot
            out[top + k:top + k + 1, :] = (rows[k] * lax.rsqrt(pivot))[:1]
            scaled = rows[k] * inv
            for a in range(k + 1, SUB):
                low = small[a, k]
                rows[a] = rows[a] - low * scaled
                low = low * inv
                for b in range(k + 1, a + 1):
                    small[a, b] = small[a, b] - low * small[b, k]
                for g in groups:
                    cols[g, a] = cols[g, a] - cols[g, k] * low
            rows[k] = scaled
        for g in groups:
            tile = work[g * SUB:(g + 1) * SUB, :]
            for k in range(SUB):
                tile = tile - cols[g, k] * rows[k]
            work[g * SUB:(g + 1) * SUB, :] = tile


def solve(me, start, diags, crosses, high, low, far, both, nx, v):
    rank = start.shape[0]
    pad = diags[0].shape[0]
    cuts = len(crosses)
    tops = [0, crosses[0][0].shape[0]]
    total = high.shape[1]
    width = total // v
    chip = nx // 2
    keep = rank // nx
    order = (0, 1, chip, chip ^ 1)

    def assemble(me_ref, d_in, c_in, gram, diag, cross):
        for s in range(nx):
            spot = me_ref[0] ^ order[s]
            diag[spot] = d_in[s][...]
            for q in range(cuts):
                cross[spot, tops[q]:tops[q] + c_in[q][s].shape[0], :] = c_in[q][s][...]
        for b in range(nx):
            at = slice(b * pad, (b + 1) * pad)
            for other, block in (
                (b, diag[b, :, :pad]),
                (b ^ 1, diag[b, :, pad:]),
                (b ^ chip, cross[b ^ chip, :, :pad] + cross[b, :, :pad].T),
                (b ^ chip ^ 1, cross[b ^ chip, :, pad:] + cross[b ^ 1, :, pad:].T),
            ):
                gram[at, other * pad:(other + 1) * pad] = block

    def iterate(s_ref, gram, work, inv, basis):
        eye_rows = lax.broadcasted_iota(jnp.int32, (rank, 2 * rank), 0)
        eye_cols = lax.broadcasted_iota(jnp.int32, (rank, 2 * rank), 1)
        eye = jnp.where(eye_rows == eye_cols, 1.0, 0.0).astype(F32)
        now = s_ref[...]
        for _ in range(ITERS):
            block = lax.dot_general(now, gram[...], NN, precision=HIGHEST, preferred_element_type=F32)
            twice = jnp.concatenate([jnp.zeros_like(block), block], 0)
            work[...] = eye + lax.dot_general(block, twice, NT, precision=HIGHEST, preferred_element_type=F32)
            inverse_factor(work, inv, rank)
            now = lax.dot_general(inv[:, :rank], block, NN, precision=HIGHEST, preferred_element_type=F32)
        for b in range(nx):
            basis[b] = now[:, b * pad:(b + 1) * pad]

    def body(me_ref, s_ref, *refs):
        d_in = refs[:nx]
        c_in = [refs[nx * (q + 1):nx * (q + 2)] for q in range(cuts)]
        refs = refs[nx * (1 + cuts):]
        h_ref, l_ref = refs[:2]
        pieces = refs[2:10]
        basis, kept, sent, gram, diag, cross, work, inv, tail_high, tail_low = refs[10:]
        for q in range(4):
            rows = slice(q // 2 * pad + tops[q % 2], q // 2 * pad + tops[q % 2] + pieces[2 * q].shape[0])
            lanes = [slice(0, pieces[2 * q].shape[1]), slice(pieces[2 * q].shape[1], total)]
            for piece, at in zip(pieces[2 * q:2 * q + 2], lanes):
                tail_high[rows, at], tail_low[rows, at] = split(piece[...])
        assemble(me_ref, d_in, c_in, gram, diag, cross)
        iterate(s_ref, gram, work, inv, basis)
        here = me_ref[0]
        parts = []
        for s in order:
            block = basis.at[here ^ s]
            ranks = [block[pl.ds(pl.multiple_of((here ^ r) * keep, keep), keep), :] for r in (0, chip)]
            parts.append(jnp.concatenate(ranks, 0))
        left = jnp.concatenate(split(jnp.concatenate(parts, 1)), 0)
        near, away = left[:, :2 * pad], left[:, 2 * pad:]
        for a in range(v):
            at = slice(a * width, (a + 1) * width)
            out = mm(near, h_ref[:, at], NN) + mm(away, tail_high[:, at], NN)
            out = out[:2 * keep] + out[2 * keep:]
            out = out + mm(near[:2 * keep], l_ref[:, at], NN) + mm(away[:2 * keep], tail_low[:, at], NN)
            kept[a] = out[:keep]
            sent[a] = out[keep:]

    shape = jax.ShapeDtypeStruct((v, keep, width), F32)
    return pl.pallas_call(
        body,
        out_shape=(jax.ShapeDtypeStruct((nx, rank, pad), F32), shape, shape),
        in_specs=[smem()] + [vmem()] * (1 + nx * (1 + cuts) + 10),
        out_specs=(vmem(), vmem(), vmem()),
        scratch_shapes=[
            pltpu.VMEM((nx * pad, nx * pad), F32),
            pltpu.VMEM((nx, pad, 2 * pad), F32),
            pltpu.VMEM((nx, pad, 2 * pad), F32),
            pltpu.VMEM((rank, 2 * rank), F32),
            pltpu.VMEM((rank, 2 * rank), F32),
            pltpu.VMEM((2 * pad, total), BF16),
            pltpu.VMEM((2 * pad, total), BF16),
        ],
        cost_estimate=cost(15),
        compiler_params=limit(SOLVE_MIB),
        name="solve",
    )(me, start, *diags, *[c for group in crosses for c in group], high, low, *far, *both)


def place(x, kept, got, j):
    v, keep, width = kept.shape
    half = j // 2
    k = width // half

    def body(x_ref, a_ref, b_ref, out):
        for data, first in ((a_ref, x_ref[0] * half), (b_ref, (1 - x_ref[0]) * half)):
            for a in range(v):
                for i in range(half):
                    out[pl.ds(a * j + first + i, keep, stride=v * j), :] = data[a, :, i * k:(i + 1) * k]

    return pl.pallas_call(
        body,
        out_shape=jax.ShapeDtypeStruct((keep * v * j, k), F32),
        in_specs=[smem(), vmem(), vmem()],
        out_specs=vmem(),
        cost_estimate=cost(2),
        compiler_params=limit(8),
        name="place",
    )(x, kept, got).reshape(keep, v, j, k)


def solution(mesh):
    sizes = dict(mesh.shape)
    nx = sizes["gx"]
    chip = nx // 2

    def swap(array, step, axis="gx"):
        return lax.ppermute(array, axis, [(i, i ^ step) for i in range(sizes[axis])])

    def sum_columns(part):
        for axis in ("gz", "gy"):
            step = 1
            while step < sizes[axis]:
                part = part + swap(part, step, axis)
                step *= 2
        return part

    def everywhere(mine):
        far = swap(mine, chip)
        return [mine, swap(mine, 1), far, swap(far, 1)]

    def program(fields, var_scale, start_basis):
        v, rows, j, k = fields.shape
        rank = start_basis.shape[1]
        pad = -(-rows // LANE) * LANE
        me = lax.axis_index("gx").reshape(1)
        x = me // chip
        flat = fields.reshape(v, rows * j, k)
        (first,) = pack(flat, var_scale, x, rows, pad, j, False)
        *rest, ours = pack(flat, var_scale, x, rows, pad, j, True)
        theirs = [first, *rest]
        far = []
        for t in theirs:
            far.append(swap(t, chip))
        near_ours = swap(ours, 1)
        near_theirs = [swap(t, 1) for t in theirs]
        high, low, diag = diagonal(ours, theirs, near_ours, near_theirs, v)
        diag = sum_columns(diag)
        diags = everywhere(diag)
        top = crossing(high, low, far[:2], None, 0)
        top = sum_columns(top)
        bottom = crossing(high, low, far[2:3], None, 0)
        bottom = crossing(high, low, far[3:], bottom, far[2].shape[1])
        crosses = [everywhere(top), everywhere(sum_columns(bottom))]
        both = [swap(f, 1) for f in far]
        start = start_basis.T.reshape(rank, nx, rows)
        start = jnp.pad(start, ((0, 0), (0, 0), (0, pad - rows))).reshape(rank, nx * pad)
        basis, kept, sent = solve(me, start, diags, crosses, high, low, far, both, nx, v)
        core = place(x, kept, swap(sent, chip), j)
        factor = basis[:, :, :rows].transpose(1, 0, 2).reshape(rank, nx * rows).T
        return factor, core

    in_specs = (P(None, "gx", "gy", "gz"), P(), P())
    out_specs = (P(), P("gx", None, "gy", "gz"))
    return jax.shard_map(program, mesh=mesh, in_specs=in_specs, out_specs=out_specs, check_vma=False)
```

time: 334 us -> 163 us (0.49)
  waiting for transfers between devices: 166 us -> 77.8 us
  blocking collectives: 69 us -> 0 us
  other arithmetic: 39.3 us -> 0.11 us
  Pallas kernels: 0 us -> 37.9 us
  matrix products: 30.5 us -> 0 us
  starting transfers between devices: 0.26 us -> 27.8 us
  between operations: 14.2 us -> 0.93 us
  local copies, waits for them, and re-layouts: 13.9 us -> 18.2 us
    psum x1 -> x0, waiting for transfers between devices: 131 us -> none  [per_device(): gram = lax.psum(partial_gram, ('gx', 'gy', 'gz'))]
    ppermute x0 -> x32, waiting for transfers between devices: none -> 77.8 us  [swap(): lax.ppermute(array, axis, [(i, i ^ step) for i in range(sizes[axis])])]
    all_to_all x1 -> x0, blocking collectives: 69 us -> none  [per_device(): lax.all_to_all(scaled, 'gx', split_axis=2, concat_axis=1, tiled=True)]
    pallas_call x0 -> x8, Pallas kernels: none -> 37.9 us  [the longest x1 12.4 us: solve(): pl.pallas_call(body, out_shape=(jax.ShapeDtypeStruct((nx, rank, pad), F32...]
    another operation x15 -> x0, other arithmetic: 36.2 us -> none  [the longest x9 19.6 us: orthonormal(): lower = jnp.linalg.cholesky(small)]
    reduce_scatter x1 -> x0, waiting for transfers between devices: 35.2 us -> none  [per_device(): lax.psum_scatter(lax.dot_general(own_basis, scaled, along_rows, precision...]
    dot_general x8 -> x0, matrix products: 29.5 us -> none  [the longest x1 13.6 us: per_device(): lax.dot_general(swapped, swapped, contract, precision=lax.Precision.HIGHEST)]
    ppermute x0 -> x32, starting transfers between devices: none -> 27.8 us  [swap(): lax.ppermute(array, axis, [(i, i ^ step) for i in range(sizes[axis])])]
  transfers between devices with their start and end apart: 2 -> 32, of which waited for: 2 -> 14; matrix products, arithmetic and copies ran while one was open for 0% -> 2% of each run, Pallas kernels for 0% -> 12%
where the time goes in v2:
time: 163 us
  waiting for transfers between devices  77.8 us (48%)
  Pallas kernels  37.9 us (23%)
  starting transfers between devices  27.8 us (17%)
  local copies, waits for them, and re-layouts  18.2 us (11%)
    ppermute x32, waiting for transfers between devices, swap(): lax.ppermute(array, axis, [(i, i ^ step) for i in range(sizes[axis])])  77.8 us
    ppermute x32, starting transfers between devices, swap(): lax.ppermute(array, axis, [(i, i ^ step) for i in range(sizes[axis])])  27.8 us
    unnamed x39, local copies, waits for them, and re-layouts  14.8 us
    pallas_call x1, Pallas kernels, solve(): pl.pallas_call(body, out_shape=(jax.ShapeDtypeStruct((nx, rank, pad), F32...  12.4 us
    pallas_call x1, Pallas kernels, diagonal(): pl.pallas_call(body, out_shape=(half, half, jax.ShapeDtypeStruct((pad, 2...  10.1 us
    pallas_call x2, Pallas kernels, pack(): pl.pallas_call(body, out_shape=shapes, in_specs=[smem(), smem(), pl.Block...  8.54 us
    pallas_call x3, Pallas kernels, crossing(): pl.pallas_call(body, out_shape=jax.ShapeDtypeStruct((cut, 2 * pad), F32),...  5.86 us
  transfers between devices with their start and end apart: 32, of which 14 were waited for; matrix products, arithmetic and copies ran while one was open for 2% of the time, Pallas kernels for 12%

profile of v2, /device:TPU:0, one launch (start us, length us, event | category | flops | bytes accessed | tf_op | source)
XLA Modules:
  0.0 162.7 jit_solution(2333490318418194452)
XLA Ops:
  1.3 5.6 %pack_rest.1 = (f32[96,3584]{1,0:T(8,128)}, f32[32,4096]{1,0:T(8,128)}, f32[32,1536]{1,0:T(8,128)}, f32[128,5632]{1,0:T(8,128)}) custom-call(s32[1]{0:T(128)S(6)} %select_n.5.x_ref, f32[11]{0:T(128)S(1)} %copy-done.12, f32[11,1000,128]{2,1,0:T(8,128)} %bitcast.15), custom_call_target="tpu_custom_call" | custom-call | flops 5000000000 | tf_op jit(solution)/shard_map/pack_rest/pallas_call | solution.py:94
  7.5 2.9 %collective-permute-start.12 = (f32[96,3584]{1,0:T(8,128)}, f32[96,3584]{1,0:T(8,128)S(1)}, u32[]{:S(2)}, u32[]{:S(2)}) collective-permute-start(f32[96,3584]{1,0:T(8,128)} %get-tuple-element.13.a2), channel_id=1, source_target_pairs={{0,16},{8,24},{16,0},{24,8},{1,17},{9,25},{17,1},{25,9},{2,18},{10... | collective-permute-start | bytes 4128776 | tf_op jit(solution)/shard_map/ppermute | solution.py:348
  10.4 3.0 %pack_first.1.a1 = f32[96,2048]{1,0:T(8,128)} custom-call(s32[1]{0:T(128)S(6)} %select_n.5.x_ref, f32[11]{0:T(128)} %s_ref.3, f32[11,1000,128]{2,1,0:T(8,128)} %bitcast.16), custom_call_target="tpu_custom_call" | custom-call | flops 2000000000 | tf_op jit(solution)/shard_map/pack_first/pallas_call | solution.py:94
  14.0 2.3 %collective-permute-done.4.d2 = f32[32,1536]{1,0:T(8,128)S(1)} collective-permute-done((f32[32,1536]{1,0:T(8,128)}, f32[32,1536]{1,0:T(8,128)S(1)}, u32[]{:S(2)}, u32[]{:S(2)}) %collective-permute-start.4) | collective-permute-done | bytes 196640 | tf_op jit(solution)/shard_map/ppermute | solution.py:348
  16.4 2.0 %collective-permute-done.3.d1 = f32[32,4096]{1,0:T(8,128)S(1)} collective-permute-done((f32[32,4096]{1,0:T(8,128)}, f32[32,4096]{1,0:T(8,128)S(1)}, u32[]{:S(2)}, u32[]{:S(2)}) %collective-permute-start.3) | collective-permute-done | bytes 524320 | tf_op jit(solution)/shard_map/ppermute | solution.py:348
  18.4 2.5 %collective-permute-start.20 = (f32[32,4096]{1,0:T(8,128)}, f32[32,4096]{1,0:T(8,128)S(1)}, u32[]{:S(2)}, u32[]{:S(2)}) collective-permute-start(f32[32,4096]{1,0:T(8,128)} %get-tuple-element.14.b1), channel_id=1, source_target_pairs={{0,16},{8,24},{16,0},{24,8},{1,17},{9,25},{17,1},{25,9},{2,18},{10... | collective-permute-start | bytes 1572872 | tf_op jit(solution)/shard_map/ppermute | solution.py:348
  20.9 2.0 %collective-permute-start.11 = (f32[96,2048]{1,0:T(8,128)}, f32[96,2048]{1,0:T(8,128)S(1)}, u32[]{:S(2)}, u32[]{:S(2)}) collective-permute-start(f32[96,2048]{1,0:T(8,128)} %pack_first.1.a1), channel_id=1, source_target_pairs={{0,16},{8,24},{16,0},{24,8},{1,17},{9,25},{17,1},{25,9},{2,18},{10... | collective-permute-start | bytes 2359304 | tf_op jit(solution)/shard_map/ppermute | solution.py:348
  22.9 18.7 %collective-permute-done.12.refs_1_.refs_15_ = f32[96,3584]{1,0:T(8,128)S(1)} collective-permute-done((f32[96,3584]{1,0:T(8,128)}, f32[96,3584]{1,0:T(8,128)S(1)}, u32[]{:S(2)}, u32[]{:S(2)}) %collective-permute-start.12) | collective-permute-done | bytes 1376288 | tf_op jit(solution)/shard_map/ppermute | solution.py:348
  42.8 10.1 %diagonal.1 = (bf16[256,5632]{1,0:T(8,128)(2,1)S(1)}, bf16[256,5632]{1,0:T(8,128)(2,1)S(1)}, f32[128,256]{1,0:T(8,128)S(1)}) custom-call(f32[128,5632]{1,0:T(8,128)S(1)} %copy-done, f32[96,2048]{1,0:T(8,128)S(1)} %copy-done.3, f32[96,3584]{1,0:T(8,128)} %get-tuple-element.13.a2, f32[32,4096]{1,0:T(8,128)} %get-tuple-element.14.b1, ...), custom_call_target="tpu_custom_call" | custom-call | flops 12000000000 | tf_op jit(solution)/shard_map/diagonal/pallas_call | solution.py:147
  52.9 20.4 %collective-permute-done.11.refs_0_.refs_14_ = f32[96,2048]{1,0:T(8,128)S(1)} collective-permute-done((f32[96,2048]{1,0:T(8,128)}, f32[96,2048]{1,0:T(8,128)S(1)}, u32[]{:S(2)}, u32[]{:S(2)}) %collective-permute-start.11) | collective-permute-done | bytes 786464 | tf_op jit(solution)/shard_map/ppermute | solution.py:348
  73.4 3.1 %crossing.3 = f32[96,256]{1,0:T(8,128)S(1)} custom-call(bf16[256,5632]{1,0:T(8,128)(2,1)S(1)} %get-tuple-element.17.h_ref.refs_12_, bf16[256,5632]{1,0:T(8,128)(2,1)S(1)} %get-tuple-element.18.l_ref.refs_13_, f32[96,2048]{1,0:T(8,128)S(1)} %collective-permute-done.11.refs_0_.refs_14_, f32[96,3584]{1,0:T(8,128)S(1)} %collective-permute-done.12.refs_1_.refs_15_), custom_call_target="tpu_custom_call" | custom-call | flops 3000000000 | tf_op jit(solution)/shard_map/crossing/pallas_call | solution.py:181
  76.4 1.8 %collective-permute-start.13 = (f32[96,256]{1,0:T(8,128)S(1)}, f32[96,256]{1,0:T(8,128)S(1)}, u32[]{:S(2)}, u32[]{:S(2)}) collective-permute-start(f32[96,256]{1,0:T(8,128)S(1)} %crossing.3), channel_id=1, source_target_pairs={{0,1},{1,0},{2,3},{3,2},{4,5},{5,4},{6,7},{7,6},{8,9},{9,8},{10,11... | collective-permute-start | bytes 294920 | tf_op jit(solution)/shard_map/ppermute | solution.py:348
  78.5 3.6 %collective-permute-done.13 = f32[96,256]{1,0:T(8,128)S(1)} collective-permute-done((f32[96,256]{1,0:T(8,128)S(1)}, f32[96,256]{1,0:T(8,128)S(1)}, u32[]{:S(2)}, u32[]{:S(2)}) %collective-permute-start.13) | collective-permute-done | bytes 98336 | tf_op jit(solution)/shard_map/ppermute | solution.py:348
  82.2 1.8 %collective-permute-start.14 = (f32[96,256]{1,0:T(8,128)S(1)}, f32[96,256]{1,0:T(8,128)S(1)}, u32[]{:S(2)}, u32[]{:S(2)}) collective-permute-start(f32[96,256]{1,0:T(8,128)S(1)} %add.33), channel_id=1, source_target_pairs={{0,2},{2,0},{4,6},{6,4},{1,3},{3,1},{5,7},{7,5},{8,10},{10,8},{12,... | collective-permute-start | bytes 294920 | tf_op jit(solution)/shard_map/ppermute | solution.py:348
  84.6 2.3 %collective-permute-done.14 = f32[96,256]{1,0:T(8,128)S(1)} collective-permute-done((f32[96,256]{1,0:T(8,128)S(1)}, f32[96,256]{1,0:T(8,128)S(1)}, u32[]{:S(2)}, u32[]{:S(2)}) %collective-permute-start.14) | collective-permute-done | bytes 98336 | tf_op jit(solution)/shard_map/ppermute | solution.py:348
  86.9 1.8 %collective-permute-start.6 = (f32[128,256]{1,0:T(8,128)S(1)}, f32[128,256]{1,0:T(8,128)S(1)}, u32[]{:S(2)}, u32[]{:S(2)}) collective-permute-start(f32[128,256]{1,0:T(8,128)S(1)} %add.30), channel_id=1, source_target_pairs={{0,2},{2,0},{4,6},{6,4},{1,3},{3,1},{5,7},{7,5},{8,10},{10,8},{12,... | collective-permute-start | bytes 393224 | tf_op jit(solution)/shard_map/ppermute | solution.py:348
  88.7 1.9 %crossing.4.refs_1_ = f32[32,256]{1,0:T(8,128)S(1)} custom-call(bf16[256,5632]{1,0:T(8,128)(2,1)S(1)} %get-tuple-element.17.h_ref.refs_12_, bf16[256,5632]{1,0:T(8,128)(2,1)S(1)} %get-tuple-element.18.l_ref.refs_13_, f32[32,4096]{1,0:T(8,128)S(1)} %collective-permute-done.20.refs_0_.refs_16_), custom_call_target="tpu_custom_call" | custom-call | flops 3000000000 | tf_op jit(solution)/shard_map/crossing/pallas_call | solution.py:181
  91.8 3.7 %collective-permute-start.15 = (f32[96,256]{1,0:T(8,128)S(1)}, f32[96,256]{1,0:T(8,128)S(1)}, u32[]{:S(2)}, u32[]{:S(2)}) collective-permute-start(f32[96,256]{1,0:T(8,128)S(1)} %add.34), channel_id=1, source_target_pairs={{0,4},{2,6},{4,0},{6,2},{1,5},{3,7},{5,1},{7,3},{8,12},{10,14},{12... | collective-permute-start | bytes 294920 | tf_op jit(solution)/shard_map/ppermute | solution.py:348
  96.6 6.3 %collective-permute-done.7 = f32[128,256]{1,0:T(8,128)S(1)} collective-permute-done((f32[128,256]{1,0:T(8,128)S(1)}, f32[128,256]{1,0:T(8,128)S(1)}, u32[]{:S(2)}, u32[]{:S(2)}) %collective-permute-start.7) | collective-permute-done | bytes 131104 | tf_op jit(solution)/shard_map/ppermute | solution.py:348
  103.0 1.3 collective-permute-start.21
  104.3 2.6 %collective-permute-done.21 = f32[32,256]{1,0:T(8,128)S(1)} collective-permute-done((f32[32,256]{1,0:T(8,128)S(1)}, f32[32,256]{1,0:T(8,128)S(1)}, u32[]{:S(2)}, u32[]{:S(2)}) %collective-permute-start.21) | collective-permute-done | bytes 32800 | tf_op jit(solution)/shard_map/ppermute | solution.py:348
  106.9 1.5 collective-permute-start.9
  108.5 3.9 %collective-permute-done.22 = f32[32,256]{1,0:T(8,128)S(1)} collective-permute-done((f32[32,256]{1,0:T(8,128)S(1)}, f32[32,256]{1,0:T(8,128)S(1)}, u32[]{:S(2)}, u32[]{:S(2)}) %collective-permute-start.22) | collective-permute-done | bytes 32800 | tf_op jit(solution)/shard_map/ppermute | solution.py:348
  115.0 3.7 %collective-permute-done.23 = f32[32,256]{1,0:T(8,128)S(1)} collective-permute-done((f32[32,256]{1,0:T(8,128)S(1)}, f32[32,256]{1,0:T(8,128)S(1)}, u32[]{:S(2)}, u32[]{:S(2)}) %collective-permute-start.23) | collective-permute-done | bytes 32800 | tf_op jit(solution)/shard_map/ppermute | solution.py:348
  119.2 1.6 collective-permute-start.25
  125.3 1.7 %reshape.27 = f32[64,4,125]{2,1,0:T(4,128)} reshape(f32[64,500]{1,0:T(8,128)} %bitcast.13) | data formatting | bytes 256000 | tf_op jit(solution)/shard_map/reshape | solution.py:386
  128.0 1.3 copy-done.2
  133.1 1.8 %copy-done.14 = bf16[256,5632]{1,0:T(8,128)(2,1)S(1)} copy-done((bf16[256,5632]{1,0:T(8,128)(2,1)S(1)}, bf16[256,5632]{1,0:T(8,128)(2,1)}, u32[]{:S(2)}) %copy-start.14) | copy-done | bytes 2883608
  134.9 1.8 %copy-done.16 = bf16[256,5632]{1,0:T(8,128)(2,1)S(1)} copy-done((bf16[256,5632]{1,0:T(8,128)(2,1)S(1)}, bf16[256,5632]{1,0:T(8,128)(2,1)}, u32[]{:S(2)}) %copy-start.16) | copy-done | bytes 2883608
  136.7 12.4 %solve.1 = (f32[4,64,128]{2,1,0:T(8,128)S(1)}, f32[11,16,512]{2,1,0:T(8,128)S(1)}, f32[11,16,512]{2,1,0:T(8,128)}) custom-call(s32[1]{0:T(128)} %bitcast.me_ref, f32[64,512]{1,0:T(8,128)S(1)} %bitcast.11, f32[128,256]{1,0:T(8,128)S(1)} %add.32.refs_0_, f32[128,256]{1,0:T(8,128)} %collective-permute-done.8.refs_1_, ...), custom_call_target="tpu_custom_call" | custom-call | flops 15000000512 | tf_op jit(solution)/shard_map/solve/pallas_call | solution.py:300
  149.9 1.5 collective-permute-start.31
  152.3 8.5 %collective-permute-done.31.b_ref = f32[11,16,512]{2,1,0:T(8,128)S(1)} collective-permute-done((f32[11,16,512]{2,1,0:T(8,128)}, f32[11,16,512]{2,1,0:T(8,128)S(1)}, u32[]{:S(2)}, u32[]{:S(2)}) %collective-permute-start.31) | collective-permute-done | bytes 360480 | tf_op jit(solution)/shard_map/ppermute | solution.py:348
  (93 shorter events, 22.4 us)
Async XLA Ops:
  6.9 34.8 %collective-permute-start = (f32[128,5632]{1,0:T(8,128)}, f32[128,5632]{1,0:T(8,128)}, u32[]{:S(2)}, u32[]{:S(2)}) collective-permute-start(f32[128,5632]{1,0:T(8,128)} %get-tuple-element.12.o_ref), channel_id=1, source_target_pairs={{0,8},{8,0},{16,24},{24,16},{1,9},{9,1},{17,25},{25,17},{2,10},{10... | collective-permute-start | bytes 8650760 | tf_op jit(solution)/shard_map/ppermute | solution.py:348
  7.4 13.5 %collective-permute-start.2 = (f32[96,3584]{1,0:T(8,128)}, f32[96,3584]{1,0:T(8,128)}, u32[]{:S(2)}, u32[]{:S(2)}) collective-permute-start(f32[96,3584]{1,0:T(8,128)} %get-tuple-element.13.a2), channel_id=1, source_target_pairs={{0,8},{8,0},{16,24},{24,16},{1,9},{9,1},{17,25},{25,17},{2,10},{10... | collective-permute-start | bytes 4128776 | tf_op jit(solution)/shard_map/ppermute | solution.py:348
  7.5 34.1 %collective-permute-start.12 = (f32[96,3584]{1,0:T(8,128)}, f32[96,3584]{1,0:T(8,128)S(1)}, u32[]{:S(2)}, u32[]{:S(2)}) collective-permute-start(f32[96,3584]{1,0:T(8,128)} %get-tuple-element.13.a2), channel_id=1, source_target_pairs={{0,16},{8,24},{16,0},{24,8},{1,17},{9,25},{17,1},{25,9},{2,18},{10... | collective-permute-start | bytes 4128776 | tf_op jit(solution)/shard_map/ppermute | solution.py:348
  13.4 7.5 %collective-permute-start.1 = (f32[96,2048]{1,0:T(8,128)}, f32[96,2048]{1,0:T(8,128)S(1)}, u32[]{:S(2)}, u32[]{:S(2)}) collective-permute-start(f32[96,2048]{1,0:T(8,128)} %pack_first.1.a1), channel_id=1, source_target_pairs={{0,8},{8,0},{16,24},{24,16},{1,9},{9,1},{17,25},{25,17},{2,10},{10... | collective-permute-start | bytes 2359304 | tf_op jit(solution)/shard_map/ppermute | solution.py:348
  13.5 2.8 %collective-permute-start.4 = (f32[32,1536]{1,0:T(8,128)}, f32[32,1536]{1,0:T(8,128)S(1)}, u32[]{:S(2)}, u32[]{:S(2)}) collective-permute-start(f32[32,1536]{1,0:T(8,128)} %get-tuple-element.15.b2), channel_id=1, source_target_pairs={{0,8},{8,0},{16,24},{24,16},{1,9},{9,1},{17,25},{25,17},{2,10},{10... | collective-permute-start | bytes 589832 | tf_op jit(solution)/shard_map/ppermute | solution.py:348
  16.2 2.1 %collective-permute-start.3 = (f32[32,4096]{1,0:T(8,128)}, f32[32,4096]{1,0:T(8,128)S(1)}, u32[]{:S(2)}, u32[]{:S(2)}) collective-permute-start(f32[32,4096]{1,0:T(8,128)} %get-tuple-element.14.b1), channel_id=1, source_target_pairs={{0,8},{8,0},{16,24},{24,16},{1,9},{9,1},{17,25},{25,17},{2,10},{10... | collective-permute-start | bytes 1572872 | tf_op jit(solution)/shard_map/ppermute | solution.py:348
  18.4 65.6 %collective-permute-start.20 = (f32[32,4096]{1,0:T(8,128)}, f32[32,4096]{1,0:T(8,128)S(1)}, u32[]{:S(2)}, u32[]{:S(2)}) collective-permute-start(f32[32,4096]{1,0:T(8,128)} %get-tuple-element.14.b1), channel_id=1, source_target_pairs={{0,16},{8,24},{16,0},{24,8},{1,17},{9,25},{17,1},{25,9},{2,18},{10... | collective-permute-start | bytes 1572872 | tf_op jit(solution)/shard_map/ppermute | solution.py:348
  20.9 63.1 %collective-permute-start.19 = (f32[32,1536]{1,0:T(8,128)}, f32[32,1536]{1,0:T(8,128)S(1)}, u32[]{:S(2)}, u32[]{:S(2)}) collective-permute-start(f32[32,1536]{1,0:T(8,128)} %get-tuple-element.15.b2), channel_id=1, source_target_pairs={{0,16},{8,24},{16,0},{24,8},{1,17},{9,25},{17,1},{25,9},{2,18},{10... | collective-permute-start | bytes 589832 | tf_op jit(solution)/shard_map/ppermute | solution.py:348
  20.9 52.4 %collective-permute-start.11 = (f32[96,2048]{1,0:T(8,128)}, f32[96,2048]{1,0:T(8,128)S(1)}, u32[]{:S(2)}, u32[]{:S(2)}) collective-permute-start(f32[96,2048]{1,0:T(8,128)} %pack_first.1.a1), channel_id=1, source_target_pairs={{0,16},{8,24},{16,0},{24,8},{1,17},{9,25},{17,1},{25,9},{2,18},{10... | collective-permute-start | bytes 2359304 | tf_op jit(solution)/shard_map/ppermute | solution.py:348
  41.7 79.2 %collective-permute-start.28 = (f32[96,3584]{1,0:T(8,128)S(1)}, f32[96,3584]{1,0:T(8,128)S(1)}, u32[]{:S(2)}, u32[]{:S(2)}) collective-permute-start(f32[96,3584]{1,0:T(8,128)S(1)} %collective-permute-done.12.refs_1_.refs_15_), channel_id=1, source_target_pairs={{0,8},{8,0},{16,24},{24,16},{1,9},{9,1},{17,25},{25,17},{2,10},{10... | collective-permute-start | bytes 4128776 | tf_op jit(solution)/shard_map/ppermute | solution.py:348
  76.4 5.7 %collective-permute-start.13 = (f32[96,256]{1,0:T(8,128)S(1)}, f32[96,256]{1,0:T(8,128)S(1)}, u32[]{:S(2)}, u32[]{:S(2)}) collective-permute-start(f32[96,256]{1,0:T(8,128)S(1)} %crossing.3), channel_id=1, source_target_pairs={{0,1},{1,0},{2,3},{3,2},{4,5},{5,4},{6,7},{7,6},{8,9},{9,8},{10,11... | collective-permute-start | bytes 294920 | tf_op jit(solution)/shard_map/ppermute | solution.py:348
  78.3 6.2 %collective-permute-start.5 = (f32[128,256]{1,0:T(8,128)S(1)}, f32[128,256]{1,0:T(8,128)S(1)}, u32[]{:S(2)}, u32[]{:S(2)}) collective-permute-start(f32[128,256]{1,0:T(8,128)S(1)} %get-tuple-element.16), channel_id=1, source_target_pairs={{0,1},{1,0},{2,3},{3,2},{4,5},{5,4},{6,7},{7,6},{8,9},{9,8},{10,11... | collective-permute-start | bytes 393224 | tf_op jit(solution)/shard_map/ppermute | solution.py:348
  82.2 4.7 %collective-permute-start.14 = (f32[96,256]{1,0:T(8,128)S(1)}, f32[96,256]{1,0:T(8,128)S(1)}, u32[]{:S(2)}, u32[]{:S(2)}) collective-permute-start(f32[96,256]{1,0:T(8,128)S(1)} %add.33), channel_id=1, source_target_pairs={{0,2},{2,0},{4,6},{6,4},{1,3},{3,1},{5,7},{7,5},{8,10},{10,8},{12,... | collective-permute-start | bytes 294920 | tf_op jit(solution)/shard_map/ppermute | solution.py:348
  83.9 35.3 %collective-permute-start.27 = (f32[96,2048]{1,0:T(8,128)S(1)}, f32[96,2048]{1,0:T(8,128)S(1)}, u32[]{:S(2)}, u32[]{:S(2)}) collective-permute-start(f32[96,2048]{1,0:T(8,128)S(1)} %collective-permute-done.11.refs_0_.refs_14_), channel_id=1, source_target_pairs={{0,8},{8,0},{16,24},{24,16},{1,9},{9,1},{17,25},{25,17},{2,10},{10... | collective-permute-start | bytes 2359304 | tf_op jit(solution)/shard_map/ppermute | solution.py:348
  84.0 11.6 %collective-permute-start.30 = (f32[32,1536]{1,0:T(8,128)S(1)}, f32[32,1536]{1,0:T(8,128)S(1)}, u32[]{:S(2)}, u32[]{:S(2)}) collective-permute-start(f32[32,1536]{1,0:T(8,128)S(1)} %collective-permute-done.19.refs_0_.refs_17_), channel_id=1, source_target_pairs={{0,8},{8,0},{16,24},{24,16},{1,9},{9,1},{17,25},{25,17},{2,10},{10... | collective-permute-start | bytes 589832 | tf_op jit(solution)/shard_map/ppermute | solution.py:348
  84.5 28.4 %collective-permute-start.29 = (f32[32,4096]{1,0:T(8,128)S(1)}, f32[32,4096]{1,0:T(8,128)S(1)}, u32[]{:S(2)}, u32[]{:S(2)}) collective-permute-start(f32[32,4096]{1,0:T(8,128)S(1)} %collective-permute-done.20.refs_0_.refs_16_), channel_id=1, source_target_pairs={{0,8},{8,0},{16,24},{24,16},{1,9},{9,1},{17,25},{25,17},{2,10},{10... | collective-permute-start | bytes 1572872 | tf_op jit(solution)/shard_map/ppermute | solution.py:348
  86.9 5.0 %collective-permute-start.6 = (f32[128,256]{1,0:T(8,128)S(1)}, f32[128,256]{1,0:T(8,128)S(1)}, u32[]{:S(2)}, u32[]{:S(2)}) collective-permute-start(f32[128,256]{1,0:T(8,128)S(1)} %add.30), channel_id=1, source_target_pairs={{0,2},{2,0},{4,6},{6,4},{1,3},{3,1},{5,7},{7,5},{8,10},{10,8},{12,... | collective-permute-start | bytes 393224 | tf_op jit(solution)/shard_map/ppermute | solution.py:348
  91.8 16.5 %collective-permute-start.15 = (f32[96,256]{1,0:T(8,128)S(1)}, f32[96,256]{1,0:T(8,128)S(1)}, u32[]{:S(2)}, u32[]{:S(2)}) collective-permute-start(f32[96,256]{1,0:T(8,128)S(1)} %add.34), channel_id=1, source_target_pairs={{0,4},{2,6},{4,0},{6,2},{1,5},{3,7},{5,1},{7,3},{8,12},{10,14},{12... | collective-permute-start | bytes 294920 | tf_op jit(solution)/shard_map/ppermute | solution.py:348
  95.6 7.3 %collective-permute-start.7 = (f32[128,256]{1,0:T(8,128)S(1)}, f32[128,256]{1,0:T(8,128)S(1)}, u32[]{:S(2)}, u32[]{:S(2)}) collective-permute-start(f32[128,256]{1,0:T(8,128)S(1)} %add.31), channel_id=1, source_target_pairs={{0,4},{2,6},{4,0},{6,2},{1,5},{3,7},{5,1},{7,3},{8,12},{10,14},{12... | collective-permute-start | bytes 393224 | tf_op jit(solution)/shard_map/ppermute | solution.py:348
  103.0 3.9 %collective-permute-start.21 = (f32[32,256]{1,0:T(8,128)S(1)}, f32[32,256]{1,0:T(8,128)S(1)}, u32[]{:S(2)}, u32[]{:S(2)}) collective-permute-start(f32[32,256]{1,0:T(8,128)S(1)} %crossing.5), channel_id=1, source_target_pairs={{0,1},{1,0},{2,3},{3,2},{4,5},{5,4},{6,7},{7,6},{8,9},{9,8},{10,11... | collective-permute-start | bytes 98312 | tf_op jit(solution)/shard_map/ppermute | solution.py:348
  106.9 11.9 %collective-permute-start.9 = (f32[128,256]{1,0:T(8,128)S(1)}, f32[128,256]{1,0:T(8,128)S(1)}, u32[]{:S(2)}, u32[]{:S(2)}) collective-permute-start(f32[128,256]{1,0:T(8,128)S(1)} %add.32.refs_0_), channel_id=1, source_target_pairs={{0,16},{8,24},{16,0},{24,8},{1,17},{9,25},{17,1},{25,9},{2,18},{10... | collective-permute-start | bytes 393224 | tf_op jit(solution)/shard_map/ppermute | solution.py:348
  108.4 4.0 %collective-permute-start.22 = (f32[32,256]{1,0:T(8,128)S(1)}, f32[32,256]{1,0:T(8,128)S(1)}, u32[]{:S(2)}, u32[]{:S(2)}) collective-permute-start(f32[32,256]{1,0:T(8,128)S(1)} %add.36), channel_id=1, source_target_pairs={{0,2},{2,0},{4,6},{6,4},{1,3},{3,1},{5,7},{7,5},{8,10},{10,8},{12,... | collective-permute-start | bytes 98312 | tf_op jit(solution)/shard_map/ppermute | solution.py:348
  112.4 9.5 %collective-permute-start.17 = (f32[96,256]{1,0:T(8,128)S(1)}, f32[96,256]{1,0:T(8,128)}, u32[]{:S(2)}, u32[]{:S(2)}) collective-permute-start(f32[96,256]{1,0:T(8,128)S(1)} %add.35.refs_4_), channel_id=1, source_target_pairs={{0,16},{8,24},{16,0},{24,8},{1,17},{9,25},{17,1},{25,9},{2,18},{10... | collective-permute-start | bytes 294920 | tf_op jit(solution)/shard_map/ppermute | solution.py:348
  113.8 5.0 %collective-permute-start.23 = (f32[32,256]{1,0:T(8,128)S(1)}, f32[32,256]{1,0:T(8,128)S(1)}, u32[]{:S(2)}, u32[]{:S(2)}) collective-permute-start(f32[32,256]{1,0:T(8,128)S(1)} %add.37), channel_id=1, source_target_pairs={{0,4},{2,6},{4,0},{6,2},{1,5},{3,7},{5,1},{7,3},{8,12},{10,14},{12... | collective-permute-start | bytes 98312 | tf_op jit(solution)/shard_map/ppermute | solution.py:348
  118.7 9.3 %collective-permute-start.8 = (f32[128,256]{1,0:T(8,128)S(1)}, f32[128,256]{1,0:T(8,128)}, u32[]{:S(2)}, u32[]{:S(2)}) collective-permute-start(f32[128,256]{1,0:T(8,128)S(1)} %add.32.refs_0_), channel_id=1, source_target_pairs={{0,8},{8,0},{16,24},{24,16},{1,9},{9,1},{17,25},{25,17},{2,10},{10... | collective-permute-start | bytes 393224 | tf_op jit(solution)/shard_map/ppermute | solution.py:348
  118.7 9.3 %collective-permute-start.10 = (f32[128,256]{1,0:T(8,128)S(1)}, f32[128,256]{1,0:T(8,128)}, u32[]{:S(2)}, u32[]{:S(2)}) collective-permute-start(f32[128,256]{1,0:T(8,128)S(1)} %collective-permute-done.9.refs_2_), channel_id=1, source_target_pairs={{0,8},{8,0},{16,24},{24,16},{1,9},{9,1},{17,25},{25,17},{2,10},{10... | collective-permute-start | bytes 393224 | tf_op jit(solution)/shard_map/ppermute | solution.py:348
  119.2 4.1 %collective-permute-start.25 = (f32[32,256]{1,0:T(8,128)S(1)}, f32[32,256]{1,0:T(8,128)}, u32[]{:S(2)}, u32[]{:S(2)}) collective-permute-start(f32[32,256]{1,0:T(8,128)S(1)} %add.38.refs_8_), channel_id=1, source_target_pairs={{0,16},{8,24},{16,0},{24,8},{1,17},{9,25},{17,1},{25,9},{2,18},{10... | collective-permute-start | bytes 98312 | tf_op jit(solution)/shard_map/ppermute | solution.py:348
  121.9 6.1 %collective-permute-start.16 = (f32[96,256]{1,0:T(8,128)S(1)}, f32[96,256]{1,0:T(8,128)}, u32[]{:S(2)}, u32[]{:S(2)}) collective-permute-start(f32[96,256]{1,0:T(8,128)S(1)} %add.35.refs_4_), channel_id=1, source_target_pairs={{0,8},{8,0},{16,24},{24,16},{1,9},{9,1},{17,25},{25,17},{2,10},{10... | collective-permute-start | bytes 294920 | tf_op jit(solution)/shard_map/ppermute | solution.py:348
  121.9 6.1 %collective-permute-start.18 = (f32[96,256]{1,0:T(8,128)}, f32[96,256]{1,0:T(8,128)}, u32[]{:S(2)}, u32[]{:S(2)}) collective-permute-start(f32[96,256]{1,0:T(8,128)} %collective-permute-done.17.refs_6_), channel_id=1, source_target_pairs={{0,8},{8,0},{16,24},{24,16},{1,9},{9,1},{17,25},{25,17},{2,10},{10... | collective-permute-start | bytes 294920 | tf_op jit(solution)/shard_map/ppermute | solution.py:348
  123.3 1.2 collective-permute-start.24
  125.1 2.8 %collective-permute-start.26 = (f32[32,256]{1,0:T(8,128)}, f32[32,256]{1,0:T(8,128)}, u32[]{:S(2)}, u32[]{:S(2)}) collective-permute-start(f32[32,256]{1,0:T(8,128)} %collective-permute-done.25.refs_10_), channel_id=1, source_target_pairs={{0,8},{8,0},{16,24},{24,16},{1,9},{9,1},{17,25},{25,17},{2,10},{10... | collective-permute-start | bytes 98312 | tf_op jit(solution)/shard_map/ppermute | solution.py:348
  149.9 10.9 %collective-permute-start.31 = (f32[11,16,512]{2,1,0:T(8,128)}, f32[11,16,512]{2,1,0:T(8,128)S(1)}, u32[]{:S(2)}, u32[]{:S(2)}) collective-permute-start(f32[11,16,512]{2,1,0:T(8,128)} %get-tuple-element.21), channel_id=1, source_target_pairs={{0,16},{8,24},{16,0},{24,8},{1,17},{9,25},{17,1},{25,9},{2,18},{10... | collective-permute-start | bytes 1081352 | tf_op jit(solution)/shard_map/ppermute | solution.py:348
  (19 other events, 152.9 us)

commit v3 on v2

--- a/solution.py
+++ b/solution.py
@@ -9,7 +9,7 @@
 ITERS = 3
 LANE = 128
 SUB = 8
-V_EARLY = 4
+V_EARLY = 2
 V_LATE = 8
 TAIL = 4
 RATE = 1e9
@@ -110,7 +110,7 @@
     pad, total = ours.shape
     width = total // v
 
-    def body(o_ref, a1, a2, b1, b2, n_ref, c1, c2, d1, d2, high, low, diag):
+    def body(o_ref, a1, a2, b1, b2, n_ref, c1, c2, d1, d2, high, low, tall_high, tall_low, diag):
         diag[...] = jnp.zeros_like(diag)
 
         def at(a):
@@ -123,11 +123,11 @@
             high_t, low_t = chip_high.T, chip_low.T
             both = mm(jnp.concatenate(own, 0), high_t, NN)
             diag[...] += both[:pad] + both[pad:] + mm(own[0], low_t, NN)
-            return chip_high, chip_low
+            return chip_high, chip_low, high_t, low_t
 
         def mine(a, carry):
             lanes = at(a)
-            high[:, lanes], low[:, lanes] = add(o_ref[:, lanes], n_ref[:, lanes])
+            high[:, lanes], low[:, lanes], tall_high[lanes, :], tall_low[lanes, :] = add(o_ref[:, lanes], n_ref[:, lanes])
             return carry
 
         lax.fori_loop(0, v, mine, 0)
@@ -144,11 +144,12 @@
             lax.fori_loop(first, last, other, 0)
 
     half = jax.ShapeDtypeStruct((2 * pad, total), BF16)
-    return pl.pallas_call(
-        body,
-        out_shape=(half, half, jax.ShapeDtypeStruct((pad, 2 * pad), F32)),
+    tall = jax.ShapeDtypeStruct((total, 2 * pad), BF16)
+    return pl.pallas_call(
+        body,
+        out_shape=(half, half, tall, tall, jax.ShapeDtypeStruct((pad, 2 * pad), F32)),
         in_specs=[vmem()] * 10,
-        out_specs=(vmem(),) * 3,
+        out_specs=(vmem(),) * 5,
         cost_estimate=cost(12),
         compiler_params=limit(DIAG_MIB),
         name="diagonal",
@@ -160,22 +161,21 @@
     return list(zip(edges[:-1], edges[1:]))
 
 
-def crossing(high, low, pieces, base, first):
+def crossing(tall_high, tall_low, pieces, base, first):
     cut = pieces[0].shape[0]
-    pad = high.shape[0] // 2
+    pad = tall_high.shape[1] // 2
 
     def body(h_ref, l_ref, *refs):
         out = refs[-1]
         spot = first
-        total = 0.0
+        total = refs[-2][...] if base is not None else 0.0
         for ref in refs[:len(pieces)]:
-            lanes = slice(spot, spot + ref.shape[1])
-            top, bottom = split(ref[...].T)
-            both = mm(h_ref[:, lanes], jnp.concatenate([top, bottom], 1), NN)
-            total = total + both[:, :cut] + both[:, cut:] + mm(l_ref[:, lanes], top, NN)
+            top, bottom = split(ref[...])
+            rows = slice(spot, spot + ref.shape[1])
+            both = mm(jnp.concatenate([top, bottom], 0), h_ref[rows, :], NN)
+            total = total + both[:cut] + both[cut:] + mm(top, l_ref[rows, :], NN)
             spot += ref.shape[1]
-        total = total.T
-        out[...] = total if base is None else refs[-2][...] + total
+        out[...] = total
 
     extra = [] if base is None else [base]
     return pl.pallas_call(
@@ -186,7 +186,22 @@
         cost_estimate=cost(3),
         compiler_params=limit(CROSS_MIB),
         name="crossing",
-    )(high, low, *pieces, *extra)
+    )(tall_high, tall_low, *pieces, *extra)
+
+
+def add(one, two, keep):
+    def body(a_ref, b_ref, *refs):
+        refs[-1][...] = a_ref[...] + b_ref[...]
+
+    return pl.pallas_call(
+        body,
+        out_shape=jax.ShapeDtypeStruct(one.shape, F32),
+        in_specs=[vmem()] * (2 + len(keep)),
+        out_specs=vmem(),
+        cost_estimate=cost(0.5),
+        compiler_params=limit(4),
+        name="add",
+    )(one, two, *keep)
 
 
 def inverse_factor(work, out, rank):
@@ -257,8 +272,10 @@
         eye_cols = lax.broadcasted_iota(jnp.int32, (rank, 2 * rank), 1)
         eye = jnp.where(eye_rows == eye_cols, 1.0, 0.0).astype(F32)
         now = s_ref[...]
+        gram_high, gram_low = split(gram[...])
         for _ in range(ITERS):
-            block = lax.dot_general(now, gram[...], NN, precision=HIGHEST, preferred_element_type=F32)
+            both = mm(jnp.concatenate(split(now), 0), gram_high, NN)
+            block = both[:rank] + both[rank:] + mm(now.astype(BF16), gram_low, NN)
             twice = jnp.concatenate([jnp.zeros_like(block), block], 0)
             work[...] = eye + lax.dot_general(block, twice, NT, precision=HIGHEST, preferred_element_type=F32)
             inverse_factor(work, inv, rank)
@@ -347,11 +364,11 @@
     def swap(array, step, axis="gx"):
         return lax.ppermute(array, axis, [(i, i ^ step) for i in range(sizes[axis])])
 
-    def sum_columns(part):
+    def sum_columns(part, keep):
         for axis in ("gz", "gy"):
             step = 1
             while step < sizes[axis]:
-                part = part + swap(part, step, axis)
+                part = add(part, swap(part, step, axis), keep)
                 step *= 2
         return part
 
@@ -374,18 +391,18 @@
             far.append(swap(t, chip))
         near_ours = swap(ours, 1)
         near_theirs = [swap(t, 1) for t in theirs]
-        high, low, diag = diagonal(ours, theirs, near_ours, near_theirs, v)
-        diag = sum_columns(diag)
+        *halves, tall_high, tall_low, diag = diagonal(ours, theirs, near_ours, near_theirs, v)
+        diag = sum_columns(diag, (*halves, tall_high, tall_low))
         diags = everywhere(diag)
-        top = crossing(high, low, far[:2], None, 0)
-        top = sum_columns(top)
-        bottom = crossing(high, low, far[2:3], None, 0)
-        bottom = crossing(high, low, far[3:], bottom, far[2].shape[1])
-        crosses = [everywhere(top), everywhere(sum_columns(bottom))]
+        top = crossing(tall_high, tall_low, far[:2], None, 0)
+        top = sum_columns(top, (*halves, tall_high, tall_low))
+        bottom = crossing(tall_high, tall_low, far[2:3], None, 0)
+        bottom = crossing(tall_high, tall_low, far[3:], bottom, far[2].shape[1])
+        crosses = [everywhere(top), everywhere(sum_columns(bottom, halves))]
         both = [swap(f, 1) for f in far]
         start = start_basis.T.reshape(rank, nx, rows)
         start = jnp.pad(start, ((0, 0), (0, 0), (0, pad - rows))).reshape(rank, nx * pad)
-        basis, kept, sent = solve(me, start, diags, crosses, high, low, far, both, nx, v)
+        basis, kept, sent = solve(me, start, diags, crosses, *halves, far, both, nx, v)
         core = place(x, kept, swap(sent, chip), j)
         factor = basis[:, :, :rows].transpose(1, 0, 2).reshape(rank, nx * rows).T
         return factor, core

time: 163 us -> 165 us (1.012)
  local copies, waits for them, and re-layouts: 18.2 us -> 27.4 us
  waiting for transfers between devices: 77.8 us -> 71.5 us
  Pallas kernels: 37.9 us -> 34.1 us
  starting transfers between devices: 27.8 us -> 30.2 us
    unnamed x39 -> x59, local copies, waits for them, and re-layouts: 14.8 us -> 23.9 us
    ppermute x32, waiting for transfers between devices: 77.8 us -> 71.5 us  [swap(): lax.ppermute(array, axis, [(i, i ^ step) for i in range(sizes[axis])])]
    ppermute x32, starting transfers between devices: 27.8 us -> 30.2 us  [swap(): lax.ppermute(array, axis, [(i, i ^ step) for i in range(sizes[axis])])]
    pallas_call x3, Pallas kernels: 5.86 us -> 3.73 us  [crossing(): pl.pallas_call(body, out_shape=jax.ShapeDtypeStruct((cut, 2 * pad), F32),...]
    pallas_call x1 -> x10, Pallas kernels: 10.1 us -> 9.5 us  [the longest x1 9.41 us: diagonal(): pl.pallas_call(body, out_shape=(half, half, tall, tall, jax.ShapeDtypeStr...]
  transfers between devices with their start and end apart: 32 -> 32, of which waited for: 14 -> 12; matrix products, arithmetic and copies ran while one was open for 2% -> 2% of each run, Pallas kernels for 12% -> 10%
where the time goes in v3:
time: 165 us; the launch traced here: 164 us
  waiting for transfers between devices  71.5 us (43%)
  Pallas kernels  34.1 us (21%)
  starting transfers between devices  30.2 us (18%)
  local copies, waits for them, and re-layouts  27.4 us (17%)
    ppermute x32, waiting for transfers between devices, swap(): lax.ppermute(array, axis, [(i, i ^ step) for i in range(sizes[axis])])  71.5 us
    ppermute x32, starting transfers between devices, swap(): lax.ppermute(array, axis, [(i, i ^ step) for i in range(sizes[axis])])  30.2 us
    unnamed x59, local copies, waits for them, and re-layouts  23.9 us
    pallas_call x1, Pallas kernels, solve(): pl.pallas_call(body, out_shape=(jax.ShapeDtypeStruct((nx, rank, pad), F32...  12.4 us
    pallas_call x1, Pallas kernels, diagonal(): pl.pallas_call(body, out_shape=(half, half, tall, tall, jax.ShapeDtypeStr...  9.41 us
    pallas_call x2, Pallas kernels, pack(): pl.pallas_call(body, out_shape=shapes, in_specs=[smem(), smem(), pl.Block...  7.5 us
    pallas_call x3, Pallas kernels, crossing(): pl.pallas_call(body, out_shape=jax.ShapeDtypeStruct((cut, 2 * pad), F32),...  3.73 us
  transfers between devices with their start and end apart: 32, of which 12 were waited for; matrix products, arithmetic and copies ran while one was open for 2% of the time, Pallas kernels for 10%

profile of v3, /device:TPU:0, one launch (start us, length us, event | category | flops | bytes accessed | tf_op | source)
XLA Modules:
  0.0 164.2 jit_solution(3586779586805943509)
XLA Ops:
  1.3 4.9 %pack_rest.1 = (f32[96,4608]{1,0:T(8,128)S(1)}, f32[32,4096]{1,0:T(8,128)S(1)}, f32[32,1536]{1,0:T(8,128)}, f32[128,5632]{1,0:T(8,128)}) custom-call(s32[1]{0:T(128)S(6)} %select_n.5.x_ref, f32[11]{0:T(128)S(1)} %copy-done.26, f32[11,1000,128]{2,1,0:T(8,128)} %bitcast.15), custom_call_target="tpu_custom_call" | custom-call | flops 5000000000 | tf_op jit(solution)/shard_map/pack_rest/pallas_call | solution.py:94
  6.9 2.9 %collective-permute-start.12 = (f32[96,4608]{1,0:T(8,128)S(1)}, f32[96,4608]{1,0:T(8,128)}, u32[]{:S(2)}, u32[]{:S(2)}) collective-permute-start(f32[96,4608]{1,0:T(8,128)S(1)} %get-tuple-element.15.a2), channel_id=1, source_target_pairs={{0,16},{8,24},{16,0},{24,8},{1,17},{9,25},{17,1},{25,9},{2,18},{10... | collective-permute-start | bytes 5308424 | tf_op jit(solution)/shard_map/ppermute | solution.py:365
  9.8 2.6 %pack_first.1.a1 = f32[96,1024]{1,0:T(8,128)} custom-call(s32[1]{0:T(128)S(6)} %select_n.5.x_ref, f32[11]{0:T(128)} %s_ref.3, f32[11,1000,128]{2,1,0:T(8,128)} %bitcast.16), custom_call_target="tpu_custom_call" | custom-call | flops 2000000000 | tf_op jit(solution)/shard_map/pack_first/pallas_call | solution.py:94
  13.0 1.9 %collective-permute-done.4.d2 = f32[32,1536]{1,0:T(8,128)} collective-permute-done((f32[32,1536]{1,0:T(8,128)}, f32[32,1536]{1,0:T(8,128)}, u32[]{:S(2)}, u32[]{:S(2)}) %collective-permute-start.4) | collective-permute-done | bytes 196640 | tf_op jit(solution)/shard_map/ppermute | solution.py:365
  14.9 2.8 %collective-permute-start.19 = (f32[32,1536]{1,0:T(8,128)}, f32[32,1536]{1,0:T(8,128)S(1)}, u32[]{:S(2)}, u32[]{:S(2)}) collective-permute-start(f32[32,1536]{1,0:T(8,128)} %get-tuple-element.17.b2), channel_id=1, source_target_pairs={{0,16},{8,24},{16,0},{24,8},{1,17},{9,25},{17,1},{25,9},{2,18},{10... | collective-permute-start | bytes 589832 | tf_op jit(solution)/shard_map/ppermute | solution.py:365
  17.7 35.1 %collective-permute-done.19.refs_0_.refs_17_ = f32[32,1536]{1,0:T(8,128)S(1)} collective-permute-done((f32[32,1536]{1,0:T(8,128)}, f32[32,1536]{1,0:T(8,128)S(1)}, u32[]{:S(2)}, u32[]{:S(2)}) %collective-permute-start.19) | collective-permute-done | bytes 196640 | tf_op jit(solution)/shard_map/ppermute | solution.py:365
  52.9 1.7 %collective-permute-start.11 = (f32[96,1024]{1,0:T(8,128)}, f32[96,1024]{1,0:T(8,128)S(1)}, u32[]{:S(2)}, u32[]{:S(2)}) collective-permute-start(f32[96,1024]{1,0:T(8,128)} %pack_first.1.a1), channel_id=1, source_target_pairs={{0,16},{8,24},{16,0},{24,8},{1,17},{9,25},{17,1},{25,9},{2,18},{10... | collective-permute-start | bytes 1179656 | tf_op jit(solution)/shard_map/ppermute | solution.py:365
  54.6 10.0 %collective-permute-done.11.refs_0_.refs_14_ = f32[96,1024]{1,0:T(8,128)S(1)} collective-permute-done((f32[96,1024]{1,0:T(8,128)}, f32[96,1024]{1,0:T(8,128)S(1)}, u32[]{:S(2)}, u32[]{:S(2)}) %collective-permute-start.11) | collective-permute-done | bytes 393248 | tf_op jit(solution)/shard_map/ppermute | solution.py:365
  64.6 1.7 %collective-permute-start.20 = (f32[32,4096]{1,0:T(8,128)S(1)}, f32[32,4096]{1,0:T(8,128)S(1)}, u32[]{:S(2)}, u32[]{:S(2)}) collective-permute-start(f32[32,4096]{1,0:T(8,128)S(1)} %get-tuple-element.16.b1), channel_id=1, source_target_pairs={{0,16},{8,24},{16,0},{24,8},{1,17},{9,25},{17,1},{25,9},{2,18},{10... | collective-permute-start | bytes 1572872 | tf_op jit(solution)/shard_map/ppermute | solution.py:365
  66.9 1.6 copy-done.3
  68.5 1.8 %copy-done.2 = f32[128,5632]{1,0:T(8,128)S(1)} copy-done((f32[128,5632]{1,0:T(8,128)S(1)}, f32[128,5632]{1,0:T(8,128)}, u32[]{:S(2)}) %copy-start.2) | copy-done | bytes 2883608
  70.4 1.8 %copy-done.4 = f32[128,5632]{1,0:T(8,128)S(1)} copy-done((f32[128,5632]{1,0:T(8,128)S(1)}, f32[128,5632]{1,0:T(8,128)}, u32[]{:S(2)}) %copy-start.4) | copy-done | bytes 2883608
  74.6 9.4 %diagonal.1 = (bf16[256,5632]{1,0:T(8,128)(2,1)S(1)}, bf16[256,5632]{1,0:T(8,128)(2,1)S(1)}, bf16[5632,256]{1,0:T(8,128)(2,1)S(1)}, bf16[5632,256]{1,0:T(8,128)(2,1)S(1)}, f32[128,256]{1,0:T(8,128)S(1)}) custom-call(f32[128,5632]{1,0:T(8,128)S(1)} %copy-done.2, f32[96,1024]{1,0:T(8,128)S(1)} %copy-done.15, f32[96,4608]{1,0:T(8,128)S(1)} %copy-done.6, ...), custom_call_target="tpu_custom_call" | custom-call | flops 12000000000 | tf_op jit(solution)/shard_map/diagonal/pallas_call | solution.py:148
  84.1 1.6 collective-permute-start.5
  85.7 2.6 %crossing.3.a_ref = f32[96,256]{1,0:T(8,128)S(1)} custom-call(bf16[5632,256]{1,0:T(8,128)(2,1)S(1)} %get-tuple-element.21.refs_2_.h_ref, bf16[5632,256]{1,0:T(8,128)(2,1)S(1)} %get-tuple-element.22.refs_3_.l_ref, f32[96,1024]{1,0:T(8,128)S(1)} %collective-permute-done.11.refs_0_.refs_14_, f32[96,4608]{1,0:T(8,128)} %collective-permute-done.12.refs_1_.refs_15_), custom_call_target="tpu_custom_call" | custom-call | flops 3000000000 | tf_op jit(solution)/shard_map/crossing/pallas_call | solution.py:181
  90.0 1.5 collective-permute-start.13
  91.5 1.6 collective-permute-start.6
  94.6 2.0 %collective-permute-done.6.b_ref = f32[128,256]{1,0:T(8,128)S(1)} collective-permute-done((f32[128,256]{1,0:T(8,128)S(1)}, f32[128,256]{1,0:T(8,128)S(1)}, u32[]{:S(2)}, u32[]{:S(2)}) %collective-permute-start.6) | collective-permute-done | bytes 131104 | tf_op jit(solution)/shard_map/ppermute | solution.py:365
  96.6 1.6 collective-permute-start.14
  98.2 2.7 %collective-permute-start.7 = (f32[128,256]{1,0:T(8,128)S(1)}, f32[128,256]{1,0:T(8,128)S(1)}, u32[]{:S(2)}, u32[]{:S(2)}) collective-permute-start(f32[128,256]{1,0:T(8,128)S(1)} %add.13.a_ref), channel_id=1, source_target_pairs={{0,4},{2,6},{4,0},{6,2},{1,5},{3,7},{5,1},{7,3},{8,12},{10,14},{12... | collective-permute-start | bytes 393224 | tf_op jit(solution)/shard_map/ppermute | solution.py:365
  102.4 3.5 %collective-permute-done.21.b_ref = f32[32,256]{1,0:T(8,128)S(1)} collective-permute-done((f32[32,256]{1,0:T(8,128)S(1)}, f32[32,256]{1,0:T(8,128)S(1)}, u32[]{:S(2)}, u32[]{:S(2)}) %collective-permute-start.21) | collective-permute-done | bytes 32800 | tf_op jit(solution)/shard_map/ppermute | solution.py:365
  105.9 1.9 %collective-permute-start.15 = (f32[96,256]{1,0:T(8,128)S(1)}, f32[96,256]{1,0:T(8,128)S(1)}, u32[]{:S(2)}, u32[]{:S(2)}) collective-permute-start(f32[96,256]{1,0:T(8,128)S(1)} %add.16.a_ref), channel_id=1, source_target_pairs={{0,4},{2,6},{4,0},{6,2},{1,5},{3,7},{5,1},{7,3},{8,12},{10,14},{12... | collective-permute-start | bytes 294920 | tf_op jit(solution)/shard_map/ppermute | solution.py:365
  107.9 1.8 %collective-permute-start.22 = (f32[32,256]{1,0:T(8,128)S(1)}, f32[32,256]{1,0:T(8,128)S(1)}, u32[]{:S(2)}, u32[]{:S(2)}) collective-permute-start(f32[32,256]{1,0:T(8,128)S(1)} %add.18.a_ref), channel_id=1, source_target_pairs={{0,2},{2,0},{4,6},{6,4},{1,3},{3,1},{5,7},{7,5},{8,10},{10,8},{12,... | collective-permute-start | bytes 98312 | tf_op jit(solution)/shard_map/ppermute | solution.py:365
  109.7 2.2 %collective-permute-done.22.b_ref = f32[32,256]{1,0:T(8,128)S(1)} collective-permute-done((f32[32,256]{1,0:T(8,128)S(1)}, f32[32,256]{1,0:T(8,128)S(1)}, u32[]{:S(2)}, u32[]{:S(2)}) %collective-permute-start.22) | collective-permute-done | bytes 32800 | tf_op jit(solution)/shard_map/ppermute | solution.py:365
  112.4 2.0 %collective-permute-start.23 = (f32[32,256]{1,0:T(8,128)S(1)}, f32[32,256]{1,0:T(8,128)S(1)}, u32[]{:S(2)}, u32[]{:S(2)}) collective-permute-start(f32[32,256]{1,0:T(8,128)S(1)} %add.19.a_ref), channel_id=1, source_target_pairs={{0,4},{2,6},{4,0},{6,2},{1,5},{3,7},{5,1},{7,3},{8,12},{10,14},{12... | collective-permute-start | bytes 98312 | tf_op jit(solution)/shard_map/ppermute | solution.py:365
  114.4 2.8 %collective-permute-done.23.b_ref = f32[32,256]{1,0:T(8,128)S(1)} collective-permute-done((f32[32,256]{1,0:T(8,128)S(1)}, f32[32,256]{1,0:T(8,128)S(1)}, u32[]{:S(2)}, u32[]{:S(2)}) %collective-permute-start.23) | collective-permute-done | bytes 32800 | tf_op jit(solution)/shard_map/ppermute | solution.py:365
  117.3 1.5 collective-permute-start.17
  120.9 2.6 %collective-permute-done.25.refs_10_ = f32[32,256]{1,0:T(8,128)S(1)} collective-permute-done((f32[32,256]{1,0:T(8,128)S(1)}, f32[32,256]{1,0:T(8,128)S(1)}, u32[]{:S(2)}, u32[]{:S(2)}) %collective-permute-start.25) | collective-permute-done | bytes 32800 | tf_op jit(solution)/shard_map/ppermute | solution.py:365
  126.3 1.7 %reshape.27 = f32[64,4,125]{2,1,0:T(4,128)} reshape(f32[64,500]{1,0:T(8,128)} %bitcast.13) | data formatting | bytes 256000 | tf_op jit(solution)/shard_map/reshape | solution.py:403
  129.0 1.8 %copy-done.1 = bf16[256,5632]{1,0:T(8,128)(2,1)S(1)} copy-done((bf16[256,5632]{1,0:T(8,128)(2,1)S(1)}, bf16[256,5632]{1,0:T(8,128)(2,1)}, u32[]{:S(2)}) %copy-start.1) | copy-done | bytes 2883608
  138.1 12.4 %solve.1 = (f32[4,64,128]{2,1,0:T(8,128)S(1)}, f32[11,16,512]{2,1,0:T(8,128)S(1)}, f32[11,16,512]{2,1,0:T(8,128)}) custom-call(s32[1]{0:T(128)} %bitcast.me_ref, f32[64,512]{1,0:T(8,128)S(1)} %bitcast.11, f32[128,256]{1,0:T(8,128)S(1)} %add.14.refs_0_, f32[128,256]{1,0:T(8,128)} %collective-permute-done.8.refs_1_, ...), custom_call_target="tpu_custom_call" | custom-call | flops 15000000512 | tf_op jit(solution)/shard_map/solve/pallas_call | solution.py:317
  152.6 9.6 %collective-permute-done.31.b_ref = f32[11,16,512]{2,1,0:T(8,128)S(1)} collective-permute-done((f32[11,16,512]{2,1,0:T(8,128)}, f32[11,16,512]{2,1,0:T(8,128)S(1)}, u32[]{:S(2)}, u32[]{:S(2)}) %collective-permute-start.31) | collective-permute-done | bytes 360480 | tf_op jit(solution)/shard_map/ppermute | solution.py:365
  (113 shorter events, 27.5 us)
Async XLA Ops:
  6.2 60.7 %collective-permute-start = (f32[128,5632]{1,0:T(8,128)}, f32[128,5632]{1,0:T(8,128)S(1)}, u32[]{:S(2)}, u32[]{:S(2)}) collective-permute-start(f32[128,5632]{1,0:T(8,128)} %get-tuple-element.14.o_ref), channel_id=1, source_target_pairs={{0,8},{8,0},{16,24},{24,16},{1,9},{9,1},{17,25},{25,17},{2,10},{10... | collective-permute-start | bytes 8650760 | tf_op jit(solution)/shard_map/ppermute | solution.py:365
  6.8 59.5 %collective-permute-start.2 = (f32[96,4608]{1,0:T(8,128)S(1)}, f32[96,4608]{1,0:T(8,128)}, u32[]{:S(2)}, u32[]{:S(2)}) collective-permute-start(f32[96,4608]{1,0:T(8,128)S(1)} %get-tuple-element.15.a2), channel_id=1, source_target_pairs={{0,8},{8,0},{16,24},{24,16},{1,9},{9,1},{17,25},{25,17},{2,10},{10... | collective-permute-start | bytes 5308424 | tf_op jit(solution)/shard_map/ppermute | solution.py:365
  6.9 60.0 %collective-permute-start.12 = (f32[96,4608]{1,0:T(8,128)S(1)}, f32[96,4608]{1,0:T(8,128)}, u32[]{:S(2)}, u32[]{:S(2)}) collective-permute-start(f32[96,4608]{1,0:T(8,128)S(1)} %get-tuple-element.15.a2), channel_id=1, source_target_pairs={{0,16},{8,24},{16,0},{24,8},{1,17},{9,25},{17,1},{25,9},{2,18},{10... | collective-permute-start | bytes 5308424 | tf_op jit(solution)/shard_map/ppermute | solution.py:365
  9.8 5.1 %collective-permute-start.4 = (f32[32,1536]{1,0:T(8,128)}, f32[32,1536]{1,0:T(8,128)}, u32[]{:S(2)}, u32[]{:S(2)}) collective-permute-start(f32[32,1536]{1,0:T(8,128)} %get-tuple-element.17.b2), channel_id=1, source_target_pairs={{0,8},{8,0},{16,24},{24,16},{1,9},{9,1},{17,25},{25,17},{2,10},{10... | collective-permute-start | bytes 589832 | tf_op jit(solution)/shard_map/ppermute | solution.py:365
  12.4 40.5 %collective-permute-start.1 = (f32[96,1024]{1,0:T(8,128)}, f32[96,1024]{1,0:T(8,128)S(1)}, u32[]{:S(2)}, u32[]{:S(2)}) collective-permute-start(f32[96,1024]{1,0:T(8,128)} %pack_first.1.a1), channel_id=1, source_target_pairs={{0,8},{8,0},{16,24},{24,16},{1,9},{9,1},{17,25},{25,17},{2,10},{10... | collective-permute-start | bytes 1179656 | tf_op jit(solution)/shard_map/ppermute | solution.py:365
  14.9 38.0 %collective-permute-start.19 = (f32[32,1536]{1,0:T(8,128)}, f32[32,1536]{1,0:T(8,128)S(1)}, u32[]{:S(2)}, u32[]{:S(2)}) collective-permute-start(f32[32,1536]{1,0:T(8,128)} %get-tuple-element.17.b2), channel_id=1, source_target_pairs={{0,16},{8,24},{16,0},{24,8},{1,17},{9,25},{17,1},{25,9},{2,18},{10... | collective-permute-start | bytes 589832 | tf_op jit(solution)/shard_map/ppermute | solution.py:365
  52.8 13.5 %collective-permute-start.3 = (f32[32,4096]{1,0:T(8,128)S(1)}, f32[32,4096]{1,0:T(8,128)S(1)}, u32[]{:S(2)}, u32[]{:S(2)}) collective-permute-start(f32[32,4096]{1,0:T(8,128)S(1)} %get-tuple-element.16.b1), channel_id=1, source_target_pairs={{0,8},{8,0},{16,24},{24,16},{1,9},{9,1},{17,25},{25,17},{2,10},{10... | collective-permute-start | bytes 1572872 | tf_op jit(solution)/shard_map/ppermute | solution.py:365
  52.9 11.7 %collective-permute-start.11 = (f32[96,1024]{1,0:T(8,128)}, f32[96,1024]{1,0:T(8,128)S(1)}, u32[]{:S(2)}, u32[]{:S(2)}) collective-permute-start(f32[96,1024]{1,0:T(8,128)} %pack_first.1.a1), channel_id=1, source_target_pairs={{0,16},{8,24},{16,0},{24,8},{1,17},{9,25},{17,1},{25,9},{2,18},{10... | collective-permute-start | bytes 1179656 | tf_op jit(solution)/shard_map/ppermute | solution.py:365
  64.6 26.9 %collective-permute-start.20 = (f32[32,4096]{1,0:T(8,128)S(1)}, f32[32,4096]{1,0:T(8,128)S(1)}, u32[]{:S(2)}, u32[]{:S(2)}) collective-permute-start(f32[32,4096]{1,0:T(8,128)S(1)} %get-tuple-element.16.b1), channel_id=1, source_target_pairs={{0,16},{8,24},{16,0},{24,8},{1,17},{9,25},{17,1},{25,9},{2,18},{10... | collective-permute-start | bytes 1572872 | tf_op jit(solution)/shard_map/ppermute | solution.py:365
  66.3 31.8 %collective-permute-start.30 = (f32[32,1536]{1,0:T(8,128)S(1)}, f32[32,1536]{1,0:T(8,128)S(1)}, u32[]{:S(2)}, u32[]{:S(2)}) collective-permute-start(f32[32,1536]{1,0:T(8,128)S(1)} %collective-permute-done.19.refs_0_.refs_17_), channel_id=1, source_target_pairs={{0,8},{8,0},{16,24},{24,16},{1,9},{9,1},{17,25},{25,17},{2,10},{10... | collective-permute-start | bytes 589832 | tf_op jit(solution)/shard_map/ppermute | solution.py:365
  66.3 52.4 %collective-permute-start.27 = (f32[96,1024]{1,0:T(8,128)S(1)}, f32[96,1024]{1,0:T(8,128)S(1)}, u32[]{:S(2)}, u32[]{:S(2)}) collective-permute-start(f32[96,1024]{1,0:T(8,128)S(1)} %collective-permute-done.11.refs_0_.refs_14_), channel_id=1, source_target_pairs={{0,8},{8,0},{16,24},{24,16},{1,9},{9,1},{17,25},{25,17},{2,10},{10... | collective-permute-start | bytes 1179656 | tf_op jit(solution)/shard_map/ppermute | solution.py:365
  66.9 62.2 %collective-permute-start.28 = (f32[96,4608]{1,0:T(8,128)}, f32[96,4608]{1,0:T(8,128)}, u32[]{:S(2)}, u32[]{:S(2)}) collective-permute-start(f32[96,4608]{1,0:T(8,128)} %collective-permute-done.12.refs_1_.refs_15_), channel_id=1, source_target_pairs={{0,8},{8,0},{16,24},{24,16},{1,9},{9,1},{17,25},{25,17},{2,10},{10... | collective-permute-start | bytes 5308424 | tf_op jit(solution)/shard_map/ppermute | solution.py:365
  84.1 5.9 %collective-permute-start.5 = (f32[128,256]{1,0:T(8,128)S(1)}, f32[128,256]{1,0:T(8,128)S(1)}, u32[]{:S(2)}, u32[]{:S(2)}) collective-permute-start(f32[128,256]{1,0:T(8,128)S(1)} %get-tuple-element.18.a_ref), channel_id=1, source_target_pairs={{0,1},{1,0},{2,3},{3,2},{4,5},{5,4},{6,7},{7,6},{8,9},{9,8},{10,11... | collective-permute-start | bytes 393224 | tf_op jit(solution)/shard_map/ppermute | solution.py:365
  90.0 4.6 %collective-permute-start.13 = (f32[96,256]{1,0:T(8,128)S(1)}, f32[96,256]{1,0:T(8,128)S(1)}, u32[]{:S(2)}, u32[]{:S(2)}) collective-permute-start(f32[96,256]{1,0:T(8,128)S(1)} %crossing.3.a_ref), channel_id=1, source_target_pairs={{0,1},{1,0},{2,3},{3,2},{4,5},{5,4},{6,7},{7,6},{8,9},{9,8},{10,11... | collective-permute-start | bytes 294920 | tf_op jit(solution)/shard_map/ppermute | solution.py:365
  91.5 5.0 %collective-permute-start.6 = (f32[128,256]{1,0:T(8,128)S(1)}, f32[128,256]{1,0:T(8,128)S(1)}, u32[]{:S(2)}, u32[]{:S(2)}) collective-permute-start(f32[128,256]{1,0:T(8,128)S(1)} %add.12.a_ref), channel_id=1, source_target_pairs={{0,2},{2,0},{4,6},{6,4},{1,3},{3,1},{5,7},{7,5},{8,10},{10,8},{12,... | collective-permute-start | bytes 393224 | tf_op jit(solution)/shard_map/ppermute | solution.py:365
  94.6 25.5 %collective-permute-start.29 = (f32[32,4096]{1,0:T(8,128)S(1)}, f32[32,4096]{1,0:T(8,128)S(1)}, u32[]{:S(2)}, u32[]{:S(2)}) collective-permute-start(f32[32,4096]{1,0:T(8,128)S(1)} %collective-permute-done.20.refs_0_.refs_16_), channel_id=1, source_target_pairs={{0,8},{8,0},{16,24},{24,16},{1,9},{9,1},{17,25},{25,17},{2,10},{10... | collective-permute-start | bytes 1572872 | tf_op jit(solution)/shard_map/ppermute | solution.py:365
  96.6 5.5 %collective-permute-start.14 = (f32[96,256]{1,0:T(8,128)S(1)}, f32[96,256]{1,0:T(8,128)S(1)}, u32[]{:S(2)}, u32[]{:S(2)}) collective-permute-start(f32[96,256]{1,0:T(8,128)S(1)} %add.15.a_ref), channel_id=1, source_target_pairs={{0,2},{2,0},{4,6},{6,4},{1,3},{3,1},{5,7},{7,5},{8,10},{10,8},{12,... | collective-permute-start | bytes 294920 | tf_op jit(solution)/shard_map/ppermute | solution.py:365
  98.2 9.7 %collective-permute-start.7 = (f32[128,256]{1,0:T(8,128)S(1)}, f32[128,256]{1,0:T(8,128)S(1)}, u32[]{:S(2)}, u32[]{:S(2)}) collective-permute-start(f32[128,256]{1,0:T(8,128)S(1)} %add.13.a_ref), channel_id=1, source_target_pairs={{0,4},{2,6},{4,0},{6,2},{1,5},{3,7},{5,1},{7,3},{8,12},{10,14},{12... | collective-permute-start | bytes 393224 | tf_op jit(solution)/shard_map/ppermute | solution.py:365
  102.0 3.9 %collective-permute-start.21 = (f32[32,256]{1,0:T(8,128)S(1)}, f32[32,256]{1,0:T(8,128)S(1)}, u32[]{:S(2)}, u32[]{:S(2)}) collective-permute-start(f32[32,256]{1,0:T(8,128)S(1)} %crossing.5.a_ref), channel_id=1, source_target_pairs={{0,1},{1,0},{2,3},{3,2},{4,5},{5,4},{6,7},{7,6},{8,9},{9,8},{10,11... | collective-permute-start | bytes 98312 | tf_op jit(solution)/shard_map/ppermute | solution.py:365
  105.9 6.5 %collective-permute-start.15 = (f32[96,256]{1,0:T(8,128)S(1)}, f32[96,256]{1,0:T(8,128)S(1)}, u32[]{:S(2)}, u32[]{:S(2)}) collective-permute-start(f32[96,256]{1,0:T(8,128)S(1)} %add.16.a_ref), channel_id=1, source_target_pairs={{0,4},{2,6},{4,0},{6,2},{1,5},{3,7},{5,1},{7,3},{8,12},{10,14},{12... | collective-permute-start | bytes 294920 | tf_op jit(solution)/shard_map/ppermute | solution.py:365
  107.9 4.0 %collective-permute-start.22 = (f32[32,256]{1,0:T(8,128)S(1)}, f32[32,256]{1,0:T(8,128)S(1)}, u32[]{:S(2)}, u32[]{:S(2)}) collective-permute-start(f32[32,256]{1,0:T(8,128)S(1)} %add.18.a_ref), channel_id=1, source_target_pairs={{0,2},{2,0},{4,6},{6,4},{1,3},{3,1},{5,7},{7,5},{8,10},{10,8},{12,... | collective-permute-start | bytes 98312 | tf_op jit(solution)/shard_map/ppermute | solution.py:365
  111.8 13.4 %collective-permute-start.9 = (f32[128,256]{1,0:T(8,128)S(1)}, f32[128,256]{1,0:T(8,128)}, u32[]{:S(2)}, u32[]{:S(2)}) collective-permute-start(f32[128,256]{1,0:T(8,128)S(1)} %add.14.refs_0_), channel_id=1, source_target_pairs={{0,16},{8,24},{16,0},{24,8},{1,17},{9,25},{17,1},{25,9},{2,18},{10... | collective-permute-start | bytes 393224 | tf_op jit(solution)/shard_map/ppermute | solution.py:365
  112.4 4.9 %collective-permute-start.23 = (f32[32,256]{1,0:T(8,128)S(1)}, f32[32,256]{1,0:T(8,128)S(1)}, u32[]{:S(2)}, u32[]{:S(2)}) collective-permute-start(f32[32,256]{1,0:T(8,128)S(1)} %add.19.a_ref), channel_id=1, source_target_pairs={{0,4},{2,6},{4,0},{6,2},{1,5},{3,7},{5,1},{7,3},{8,12},{10,14},{12... | collective-permute-start | bytes 98312 | tf_op jit(solution)/shard_map/ppermute | solution.py:365
  117.3 9.1 %collective-permute-start.17 = (f32[96,256]{1,0:T(8,128)S(1)}, f32[96,256]{1,0:T(8,128)}, u32[]{:S(2)}, u32[]{:S(2)}) collective-permute-start(f32[96,256]{1,0:T(8,128)S(1)} %add.17.refs_4_), channel_id=1, source_target_pairs={{0,16},{8,24},{16,0},{24,8},{1,17},{9,25},{17,1},{25,9},{2,18},{10... | collective-permute-start | bytes 294920 | tf_op jit(solution)/shard_map/ppermute | solution.py:365
  119.6 3.9 %collective-permute-start.25 = (f32[32,256]{1,0:T(8,128)S(1)}, f32[32,256]{1,0:T(8,128)S(1)}, u32[]{:S(2)}, u32[]{:S(2)}) collective-permute-start(f32[32,256]{1,0:T(8,128)S(1)} %add.20.refs_8_), channel_id=1, source_target_pairs={{0,16},{8,24},{16,0},{24,8},{1,17},{9,25},{17,1},{25,9},{2,18},{10... | collective-permute-start | bytes 98312 | tf_op jit(solution)/shard_map/ppermute | solution.py:365
  120.9 3.2 %collective-permute-start.24 = (f32[32,256]{1,0:T(8,128)S(1)}, f32[32,256]{1,0:T(8,128)S(1)}, u32[]{:S(2)}, u32[]{:S(2)}) collective-permute-start(f32[32,256]{1,0:T(8,128)S(1)} %add.20.refs_8_), channel_id=1, source_target_pairs={{0,8},{8,0},{16,24},{24,16},{1,9},{9,1},{17,25},{25,17},{2,10},{10... | collective-permute-start | bytes 98312 | tf_op jit(solution)/shard_map/ppermute | solution.py:365
  123.5 1.7 %collective-permute-start.26 = (f32[32,256]{1,0:T(8,128)S(1)}, f32[32,256]{1,0:T(8,128)S(1)}, u32[]{:S(2)}, u32[]{:S(2)}) collective-permute-start(f32[32,256]{1,0:T(8,128)S(1)} %collective-permute-done.25.refs_10_), channel_id=1, source_target_pairs={{0,8},{8,0},{16,24},{24,16},{1,9},{9,1},{17,25},{25,17},{2,10},{10... | collective-permute-start | bytes 98312 | tf_op jit(solution)/shard_map/ppermute | solution.py:365
  124.7 4.3 %collective-permute-start.8 = (f32[128,256]{1,0:T(8,128)S(1)}, f32[128,256]{1,0:T(8,128)}, u32[]{:S(2)}, u32[]{:S(2)}) collective-permute-start(f32[128,256]{1,0:T(8,128)S(1)} %add.14.refs_0_), channel_id=1, source_target_pairs={{0,8},{8,0},{16,24},{24,16},{1,9},{9,1},{17,25},{25,17},{2,10},{10... | collective-permute-start | bytes 393224 | tf_op jit(solution)/shard_map/ppermute | solution.py:365
  125.2 3.8 %collective-permute-start.10 = (f32[128,256]{1,0:T(8,128)}, f32[128,256]{1,0:T(8,128)}, u32[]{:S(2)}, u32[]{:S(2)}) collective-permute-start(f32[128,256]{1,0:T(8,128)} %collective-permute-done.9.refs_2_), channel_id=1, source_target_pairs={{0,8},{8,0},{16,24},{24,16},{1,9},{9,1},{17,25},{25,17},{2,10},{10... | collective-permute-start | bytes 393224 | tf_op jit(solution)/shard_map/ppermute | solution.py:365
  125.8 3.2 %collective-permute-start.16 = (f32[96,256]{1,0:T(8,128)S(1)}, f32[96,256]{1,0:T(8,128)}, u32[]{:S(2)}, u32[]{:S(2)}) collective-permute-start(f32[96,256]{1,0:T(8,128)S(1)} %add.17.refs_4_), channel_id=1, source_target_pairs={{0,8},{8,0},{16,24},{24,16},{1,9},{9,1},{17,25},{25,17},{2,10},{10... | collective-permute-start | bytes 294920 | tf_op jit(solution)/shard_map/ppermute | solution.py:365
  126.3 2.7 %collective-permute-start.18 = (f32[96,256]{1,0:T(8,128)}, f32[96,256]{1,0:T(8,128)}, u32[]{:S(2)}, u32[]{:S(2)}) collective-permute-start(f32[96,256]{1,0:T(8,128)} %collective-permute-done.17.refs_6_), channel_id=1, source_target_pairs={{0,8},{8,0},{16,24},{24,16},{1,9},{9,1},{17,25},{25,17},{2,10},{10... | collective-permute-start | bytes 294920 | tf_op jit(solution)/shard_map/ppermute | solution.py:365
  151.2 11.1 %collective-permute-start.31 = (f32[11,16,512]{2,1,0:T(8,128)}, f32[11,16,512]{2,1,0:T(8,128)S(1)}, u32[]{:S(2)}, u32[]{:S(2)}) collective-permute-start(f32[11,16,512]{2,1,0:T(8,128)} %get-tuple-element.25), channel_id=1, source_target_pairs={{0,16},{8,24},{16,0},{24,8},{1,17},{9,25},{17,1},{25,9},{2,18},{10... | collective-permute-start | bytes 1081352 | tf_op jit(solution)/shard_map/ppermute | solution.py:365
  (29 other events, 85.5 us)
